TPU v7x, 32 devices: a whole 2x2x4 slice. The times are simulated.
32 devices in a mesh: dp: 32 (over z, y, x, core).
Axes of the slice: x: 2, y: 2, z: 4, core: 2. Of those that a mesh axis runs over, the one named last changes fastest.
Arguments:
- attn_grad: bfloat16 [32, 4, 1024, 1024], P('dp')
- attn_weight: float32 [4, 1024, 1024], P(None, 'dp')
- attn_row: float32 [4, 1024], P(None, 'dp')
- attn_col: float32 [4, 1024], replicated
- ffin_grad: bfloat16 [32, 1024, 512], P('dp')
- ffin_weight: float32 [1024, 512], P('dp')
- ffin_row: float32 [1024], P('dp')
- ffin_col: float32 [512], replicated
- ffout_grad: bfloat16 [32, 512, 1024], P('dp')
- ffout_weight: float32 [512, 1024], P('dp')
- ffout_row: float32 [512], P('dp')
- ffout_col: float32 [1024], replicated
- exin_grad: float32 [32, 1024, 512], P('dp')
- exin_weight: float32 [32, 1024, 512], P('dp')
- exin_row: float32 [32, 1024], P('dp')
- exin_col: float32 [32, 512], P('dp')
- exout_grad: float32 [32, 512, 1024], P('dp')
- exout_weight: float32 [32, 512, 1024], P('dp')
- exout_row: float32 [32, 512], P('dp')
- exout_col: float32 [32, 1024], P('dp')
Outputs:
- output 1: float32 [4, 1024, 1024], P(None, 'dp')
- output 2: float32 [4, 1024], P(None, 'dp')
- output 3: float32 [4, 1024], replicated
- output 4: float32 [1024, 512], P('dp')
- output 5: float32 [1024], P('dp')
- output 6: float32 [512], replicated
- output 7: float32 [512, 1024], P('dp')
- output 8: float32 [512], P('dp')
- output 9: float32 [1024], replicated
- output 10: float32 [32, 1024, 512], P('dp')
- output 11: float32 [32, 1024], P('dp')
- output 12: float32 [32, 512], P('dp')
- output 13: float32 [32, 512, 1024], P('dp')
- output 14: float32 [32, 512], P('dp')
- output 15: float32 [32, 1024], P('dp')
All inputs are finite; a program needn't handle non-finite values.
Results may differ from a plain program's by a relative error of at most 0.001.
Values sent between devices are 32-bit elements.
A program may use at most 1 GiB of HBM per device.

v0:
```python
import jax
import jax.numpy as jnp
from jax import lax
from jax.sharding import PartitionSpec as P

OPT_STEP = 10
LEARN_RATE = 0.1
EPS_SQUARE = 1e-30
EPS_SCALE = 1e-3
CLIP_LIMIT = 1.0
BETA_TWO = 1.0 - OPT_STEP ** -0.8


def dp_total(value, across):
    return lax.psum(value, "dp") if across else value


def factored_step(gradient, weight, row_state, col_state, n_shards):
    across = n_shards > 1
    n_rows = gradient.shape[-2] * n_shards
    n_elems = n_rows * gradient.shape[-1]
    square = gradient * gradient + EPS_SQUARE
    row_new = BETA_TWO * row_state + (1.0 - BETA_TWO) * jnp.mean(square, axis=-1)
    col_sum = dp_total(jnp.sum(square, axis=-2), across)
    col_new = BETA_TWO * col_state + (1.0 - BETA_TWO) * (col_sum / n_rows)
    row_mean = dp_total(jnp.sum(row_new, axis=-1), across) / n_rows
    row_factor = lax.rsqrt(row_new / row_mean[..., None])
    update = gradient * row_factor[..., :, None] * lax.rsqrt(col_new)[..., None, :]
    upd_rms = jnp.sqrt(dp_total(jnp.sum(update * update, axis=(-2, -1)), across) / n_elems)
    w_rms = jnp.sqrt(dp_total(jnp.sum(weight * weight, axis=(-2, -1)), across) / n_elems)
    step_coeff = LEARN_RATE * jnp.maximum(EPS_SCALE, w_rms) / jnp.maximum(1.0, upd_rms / CLIP_LIMIT)
    return weight - step_coeff[..., None, None] * update, row_new, col_new


def solution(mesh):
    n_dev = mesh.shape["dp"]
    dense_specs = (
        (P("dp"), P(None, "dp", None), P(None, "dp"), P()),
        (P("dp"), P("dp", None), P("dp"), P()),
        (P("dp"), P("dp", None), P("dp"), P()),
    )
    expert_specs = ((P("dp"), P("dp"), P("dp"), P("dp")),) * 2
    all_specs = dense_specs + expert_specs
    in_specs = tuple(part_spec for group in all_specs for part_spec in group)
    out_specs = tuple(part_spec for group in all_specs for part_spec in group[1:])

    def update_all(*arrays):
        results = []
        for index, row_dim in enumerate((1, 0, 0)):
            grad_local, weight, row_state, col_state = arrays[4 * index: 4 * index + 4]
            summed = lax.psum_scatter(grad_local[0].astype(jnp.float32), "dp", scatter_dimension=row_dim, tiled=True)
            results.extend(factored_step(summed / n_dev, weight, row_state, col_state, n_dev))
        for index in (3, 4):
            gradient, weight, row_state, col_state = arrays[4 * index: 4 * index + 4]
            results.extend(factored_step(gradient, weight, row_state, col_state, 1))
        return tuple(results)

    return jax.shard_map(update_all, mesh=mesh, in_specs=in_specs, out_specs=out_specs, check_vma=False)
```

profile of v0, /device:TPU:0, one launch (start us, length us, event | category | flops | bytes accessed | tf_op | source)
XLA Modules:
  0.0 575.9 jit_solution(1501339286877382776)
XLA Ops:
  7.2 2.9 bitcast_convert_fusion.1
  10.2 1.6 bitcast_convert_fusion.2
  11.9 11.3 %bitcast_convert_fusion = f32[4,1024,1024]{2,1,0:T(8,128)} fusion(bf16[1,4,1024,1024]{3,2,1,0:T(8,128)(2,1)} %param.20), kind=kLoop, calls=%fused_computation | loop fusion | flops 4194304 | bytes 25165824 | tf_op jit(solution)/shard_map/convert_element_type | solution.py:51
  23.2 1.6 copy-done
  25.2 1.2 copy-done.1
  26.8 1.2 fusion.11
  28.7 1.2 fusion.10
  29.9 1.3 multiply_reduce_fusion.2
  31.9 2.7 multiply_reduce_fusion.3
  36.0 2.9 multiply_reduce_fusion
  39.6 2.7 multiply_reduce_fusion.1
  43.2 0.6 multiply_reduce_fusion.7
  43.8 0.6 multiply_reduce_fusion.9
  44.6 3.3 multiply_subtract_fusion.1
  47.9 103.6 %reduce-scatter.8.cloned.1.call-done = f32[16,1024]{1,0:T(8,128)} async-done(((f32[512,1024]{1,0:T(8,128)}), f32[16,1024]{1,0:T(8,128)}) %reduce-scatter.8.cloned.1.call-update) | async-done | bytes 65552 | tf_op jit(solution)/shard_map/reduce_scatter | solution.py:51
  151.5 1.0 fusion.9
  152.5 136.2 %reduce-scatter.6.cloned.1.call-done = f32[32,512]{1,0:T(8,128)} async-done(((f32[1024,512]{1,0:T(8,128)}), f32[32,512]{1,0:T(8,128)}) %reduce-scatter.6.cloned.1.call-update) | async-done | bytes 65552 | tf_op jit(solution)/shard_map/reduce_scatter | solution.py:51
  288.6 1.0 fusion.7
  289.6 0.6 fusion.17
  290.2 0.6 fusion.18
  290.8 178.7 %reduce-scatter.4.cloned.1.call-done = f32[4,32,1024]{2,1,0:T(8,128)} async-done(((f32[4,1024,1024]{2,1,0:T(8,128)}), f32[4,32,1024]{2,1,0:T(8,128)}) %reduce-scatter.4.cloned.1.call-update) | async-done | bytes 524304 | tf_op jit(solution)/shard_map/reduce_scatter | solution.py:51
  469.6 1.2 fusion.5
  470.9 42.9 %all-reduce.1 = (f32[4,1024]{1,0:T(4,128)S(1)}, f32[4]{0:T(128)S(1)}, f32[512]{0:T(512)S(1)}, f32[]{:T(128)}, f32[1024]{0:T(1024)S(1)}, /*index=5*/f32[]{:T(128)}) all-reduce(f32[4,1024]{1,0:T(4,128)S(1)} %get-tuple-element.20, f32[4]{0:T(128)S(1)} %get-tuple-element.55, ...), channel_id=1, replica_groups=mesh['dp'=32] {'dp'}, use_global_device_ids=true, to_apply=%region_7.0 | all-reduce | flops 5638 | bytes 45104 | tf_op jit(solution)/shard_map/psum | solution.py:15
  516.4 0.6 fusion.16
  517.0 1.6 multiply_reduce_fusion.6
  518.7 1.5 multiply_reduce_fusion.8
  520.2 1.3 multiply_reduce_fusion.4
  521.5 4.0 multiply_subtract_fusion
  525.5 38.6 %all-reduce = (f32[4]{0:T(128)S(1)}, f32[4]{0:T(128)S(1)}, f32[]{:T(128)}, f32[]{:T(128)}, f32[]{:T(128)}, /*index=5*/f32[]{:T(128)}) all-reduce(f32[4]{0:T(128)S(1)} %multiply_reduce_fusion.4, f32[4]{0:T(128)S(1)} %multiply_reduce_fusion.5, f32[]{:T(128)} %multiply_reduce_fusion.9, ...), channel_id=1, replica_groups=mesh['dp'=32] {'dp'}, use_global_device_ids=true, to_apply=%region_9.0 | all-reduce | flops 12 | bytes 96 | tf_op jit(solution)/shard_map/psum | solution.py:15
  567.0 0.7 multiply_subtract_fusion.3
  567.7 0.7 multiply_subtract_fusion.4
  568.5 0.9 multiply_subtract_fusion.2
  (69 shorter events, 2.7 us)
Async XLA Ops:
  7.2 3.0 copy-start.4
  7.2 144.3 %reduce-scatter.8.cloned.1.call-start = ((), (), s32[]{:S(2)}) async-start(), calls=%async_computation.5 | async-start | bytes 2162688 | tf_op jit(solution)/shard_map/reduce_scatter | solution.py:51
  10.2 278.5 %reduce-scatter.6.cloned.1.call-start = ((), (), s32[]{:S(2)}) async-start(), calls=%async_computation.4 | async-start | bytes 2162688 | tf_op jit(solution)/shard_map/reduce_scatter | solution.py:51
  11.9 457.7 %reduce-scatter.4.cloned.1.call-start = ((), (), s32[]{:S(2)}) async-start(), calls=%async_computation.3 | async-start | bytes 17301504 | tf_op jit(solution)/shard_map/reduce_scatter | solution.py:51
  23.2 1.6 copy-start
  24.8 1.6 copy-start.1
  24.8 2.0 copy-start.13
  24.8 2.0 copy-start.14
  24.8 4.0 copy-start.18
  24.8 4.0 copy-start.19
  28.0 6.6 %copy-start.9 = (f32[1,1024]{1,0:T(1,128)}, f32[1,1024]{1,0:T(1,128)S(1)}, u32[]{:S(2)}) copy-start(f32[1,1024]{1,0:T(1,128)S(1)} %get-tuple-element.60) | copy-start | bytes 12292
  29.9 6.1 %copy-start.12 = (f32[1,512]{1,0:T(1,128)}, f32[1,512]{1,0:T(1,128)S(1)}, u32[]{:S(2)}) copy-start(f32[1,512]{1,0:T(1,128)S(1)} %get-tuple-element.38) | copy-start | bytes 6148
  36.0 7.2 %copy-start.7 = (f32[16,1024]{1,0:T(8,128)S(1)}, f32[16,1024]{1,0:T(8,128)}, u32[]{:S(2)}) copy-start(f32[16,1024]{1,0:T(8,128)} %param.29) | copy-start | bytes 196612
  36.0 7.8 %copy-start.8 = (f32[32,512]{1,0:T(8,128)S(1)}, f32[32,512]{1,0:T(8,128)}, u32[]{:S(2)}) copy-start(f32[32,512]{1,0:T(8,128)} %param.25) | copy-start | bytes 196612
  36.0 8.4 %copy-start.3 = (f32[4,32,1024]{2,1,0:T(8,128)S(1)}, f32[4,32,1024]{2,1,0:T(8,128)}, u32[]{:S(2)}) copy-start(f32[4,32,1024]{2,1,0:T(8,128)} %param.21) | copy-start | bytes 1572868
  44.5 245.1 %copy-start.20 = (f32[16]{0:T(128)S(1)}, f32[16]{0:T(128)}, u32[]{:S(2)}) copy-start(f32[16]{0:T(128)} %param.30) | copy-start | bytes 196
  44.6 245.7 %copy-start.21 = (f32[32]{0:T(128)S(1)}, f32[32]{0:T(128)}, u32[]{:S(2)}) copy-start(f32[32]{0:T(128)} %param.26) | copy-start | bytes 388
  44.6 426.2 %copy-start.16 = (f32[4,32]{1,0:T(4,128)S(1)}, f32[4,32]{1,0:T(4,128)}, u32[]{:S(2)}) copy-start(f32[4,32]{1,0:T(4,128)} %param.22) | copy-start | bytes 1540
  44.6 470.6 %copy-start.15 = (f32[1024]{0:T(1024)S(1)}, f32[1024]{0:T(1024)}, u32[]{:S(2)}) copy-start(f32[1024]{0:T(1024)} %param.31) | copy-start | bytes 12292
  44.6 471.2 %copy-start.17 = (f32[512]{0:T(512)S(1)}, f32[512]{0:T(512)}, u32[]{:S(2)}) copy-start(f32[512]{0:T(512)} %param.27) | copy-start | bytes 6148
  44.6 471.8 %copy-start.10 = (f32[4,1024]{1,0:T(4,128)S(1)}, f32[4,1024]{1,0:T(4,128)}, u32[]{:S(2)}) copy-start(f32[4,1024]{1,0:T(4,128)} %param.23) | copy-start | bytes 49156
  290.2 235.3 %copy-start.22 = (f32[16]{0:T(128)}, f32[16]{0:T(128)S(1)}, u32[]{:S(2)}) copy-start(f32[16]{0:T(128)S(1)} %get-tuple-element.52) | copy-start | bytes 196
  290.8 234.7 %copy-start.23 = (f32[32]{0:T(128)}, f32[32]{0:T(128)S(1)}, u32[]{:S(2)}) copy-start(f32[32]{0:T(128)S(1)} %get-tuple-element.54) | copy-start | bytes 388
  470.9 54.6 %copy-start.11 = (f32[4,32]{1,0:T(4,128)}, f32[4,32]{1,0:T(4,128)S(1)}, u32[]{:S(2)}) copy-start(f32[4,32]{1,0:T(4,128)S(1)} %get-tuple-element.56) | copy-start | bytes 1540
  521.5 45.6 %copy-start.5 = (f32[16,1024]{1,0:T(8,128)S(1)}, f32[16,1024]{1,0:T(8,128)}, u32[]{:S(2)}) copy-start(f32[16,1024]{1,0:T(8,128)} %reduce-scatter.8.cloned.1.call-done) | copy-start | bytes 196612
  521.5 46.3 %copy-start.6 = (f32[32,512]{1,0:T(8,128)S(1)}, f32[32,512]{1,0:T(8,128)}, u32[]{:S(2)}) copy-start(f32[32,512]{1,0:T(8,128)} %reduce-scatter.6.cloned.1.call-done) | copy-start | bytes 196612
  521.5 47.0 %copy-start.2 = (f32[4,32,1024]{2,1,0:T(8,128)S(1)}, f32[4,32,1024]{2,1,0:T(8,128)}, u32[]{:S(2)}) copy-start(f32[4,32,1024]{2,1,0:T(8,128)} %reduce-scatter.4.cloned.1.call-done) | copy-start | bytes 1572868
Sparse Core Ops, SparseCore 0:
  10.3 141.1 reduce-scatter.7
  154.3 134.2 reduce-scatter.5
  290.9 178.5 reduce-scatter.3
where the time goes:
time: 577 us; the launch traced here: 576 us
  waiting for transfers between devices  419 us (73%)
  blocking collectives  81.5 us (14%)
  other arithmetic  50.5 us (9%)
  between operations  22.4 us (4%)
    reduce_scatter x3, waiting for transfers between devices, update_all(): lax.psum_scatter(grad_local[0].astype(jnp.float32), 'dp', scatter_dimensi...  418 us
    psum x2, blocking collectives, dp_total(): return lax.psum(value, 'dp') if across else value  81.5 us
    convert_element_type x3, other arithmetic, update_all(): grad_local[0].astype(jnp.float32)  15.8 us
  transfers between devices with their start and end apart: 3, of which 3 were waited for; matrix products, arithmetic and copies ran while one was open for 6% of the time, Pallas kernels for 0%

commit v1 on v0

v1 whole, which is shorter than its diff:
```python
import jax
import jax.numpy as jnp
from jax import lax
from jax.experimental import pallas as pl
from jax.experimental.pallas import tpu as pltpu
from jax.sharding import PartitionSpec as P

OPT_STEP = 10
LEARN_RATE = 0.1
EPS_SQUARE = 1e-30
EPS_SCALE = 1e-3
BETA_TWO = 1.0 - OPT_STEP ** -0.8
KEEP = 1.0 - BETA_TWO
F32 = jnp.float32
BLK_R, BLK_C = 16, 512
N_UNITS = 20
BIT = {"x": 1, "y": 2, "a": 3, "b": 4}

ORDERS = ("xayb", "yaxb") * 10
STEP_UNITS = (
    0, 1, 2, 0, 3, 1, 4, 5, 6, 7, 8, 9, 2, 10, 3, 11, 12, 0, 13, 14, 15, 16, 1, 4,
    17, 5, 18, 19, 2, 3, 1, 0, 6, 2, 4, 7, 5, 0, 3, 1, 8, 4, 6, 0, 9, 2, 1, 7,
    5, 3, 2, 10, 6, 8, 11, 4, 3, 9, 7, 5, 4, 12, 8, 10, 13, 6, 5, 11, 9, 7, 6, 14,
    10, 12, 15, 8, 7, 13, 11, 9, 8, 16, 12, 14, 17, 10, 9, 15, 13, 11, 10, 12, 18, 14, 16, 19,
    11, 12, 17, 15, 13, 14, 16, 18, 13, 17, 14, 19, 15, 16, 18, 17, 15, 19, 16, 18, 17, 19, 18, 19,
)
STEPS = [(u, STEP_UNITS[:n].count(u)) for n, u in enumerate(STEP_UNITS)]

UNITS = [(m, 16 * r, 512 * c) for m in range(4) for r in range(2) for c in range(2)]
UNITS += [(4, 0, 0), (4, 16, 0), (5, 0, 0), (5, 0, 512)]
N_ROWS = (1024, 1024, 1024, 1024, 1024, 512)
N_COLS = (1024, 1024, 1024, 1024, 512, 1024)
LOC_ROWS = (32, 32, 32, 32, 32, 16)
ROW_AT = (0, 32, 64, 96, 128, 160)
GROUP_AT = (0, 8, 16, 24, 32, 36)
MESH = pl.DeviceIdType.MESH


def sum_all(value):
    return jnp.sum(jnp.sum(value, axis=1, keepdims=True), axis=0, keepdims=True)


def dense_kernel(attn_g, ffin_g, ffout_g, attn_w, ffin_w, ffout_w, attn_r, ffin_r, ffout_r, col_in,
                 gsum, row_out, stat_out,
                 raw, stage, r0, r1, r2, r3, r4, msg, rx, tile, rb, ld_sem, s_sem, r_sem, x_sem):
    me = lax.axis_index("dp")
    bits = [(me // 2 ** k) % 2 for k in range(5)]
    partner = [me + (1 - 2 * bits[k]) * 2 ** k for k in range(5)]
    core = bits[0]
    recvs = (r0, r1, r2, r3, r4)

    def source(u):
        m, row, col = UNITS[u]
        if m < 4:
            return attn_g.at[m, :, pl.ds(row, BLK_R), pl.ds(col, BLK_C)]
        ref = ffin_g if m == 4 else ffout_g
        return ref.at[:, pl.ds(row, BLK_R), pl.ds(col, BLK_C)]

    loads = [pltpu.make_async_copy(source(u), raw.at[u], ld_sem.at[u]) for u in range(N_UNITS)]
    for load in loads:
        load.start()

    def dest(order, i):
        return sum(((i // 2 ** (3 - j)) % 2) * 2 ** BIT[order[j]] for j in range(4))

    def copy(u, s):
        order = ORDERS[u]
        if s == 0:
            src, to = stage.at[u], partner[0]
        else:
            keep = sum(bits[BIT[order[j]]] * 2 ** (3 - j) for j in range(s - 1))
            k = BIT[order[s - 1]]
            src = r0.at[u, pl.ds(keep + (1 - bits[k]) * 2 ** (4 - s), 2 ** (4 - s))]
            to = partner[k]
        return pltpu.make_async_remote_copy(
            src_ref=src, dst_ref=recvs[s].at[u], send_sem=s_sem.at[s, u], recv_sem=r_sem.at[s, u],
            device_id=(to,), device_id_type=MESH)

    def block_sum(u, s, i, d):
        total = raw[u, d].astype(F32)
        for j in range(s):
            total = total + recvs[j][u, i % 2 ** (4 - j)]
        return total

    def step(u, s):
        order = ORDERS[u]
        if s == 0:
            loads[u].wait()

            @pl.loop(0, 16)
            def _(i):
                stage[u, i] = raw[u, dest(order, i) + 1 - core].astype(F32)
        else:
            copy(u, s - 1).wait_recv()
            base = sum(bits[BIT[order[j]]] * 2 ** (3 - j) for j in range(min(s - 1, 4)))
            if s == 5:
                gsum[u] = block_sum(u, 5, base, me) * (1.0 / 32.0)
                return
            base = base + (1 - bits[BIT[order[s - 1]]]) * 2 ** (4 - s)

            @pl.loop(0, 2 ** (4 - s))
            def _(n):
                i = base + n
                r0[u, i] = block_sum(u, s, i, dest(order, i) + core)
        copy(u, s).start()

    for u, s in STEPS:
        step(u, s)

    rows_in = (attn_r, attn_r, attn_r, attn_r, ffin_r, ffout_r)
    weights = (attn_w, attn_w, attn_w, attn_w, ffin_w, ffout_w)
    lane = lax.broadcasted_iota(jnp.int32, (1, 128), 1)
    scalars = jnp.zeros((1, 128), F32)
    msg[...] = jnp.zeros((32, 8, 128), F32)
    for m in range(6):
        units = [u for u in range(N_UNITS) if UNITS[u][0] == m]
        n_loc, n_col = LOC_ROWS[m], N_COLS[m]
        col_s = [0.0] * (n_col // 512)
        col_d = [0.0] * (n_col // 512)
        new_rows = []
        total = jnp.zeros((1, 1), F32)
        for h in range(n_loc // 16):
            here = [u for u in units if UNITS[u][1] == 16 * h]
            squares = {u: gsum[u] * gsum[u] for u in here}
            row_sum = sum(jnp.sum(squares[u] + EPS_SQUARE, axis=1, keepdims=True) for u in here)
            old = rows_in[m][m, :] if m < 4 else rows_in[m][0, :]
            pick = lax.broadcasted_iota(jnp.int32, (16, n_loc), 0) + 16 * h == lax.broadcasted_iota(
                jnp.int32, (16, n_loc), 1)
            old_col = jnp.sum(jnp.where(pick, jnp.broadcast_to(old.reshape(1, n_loc), (16, n_loc)), 0.0),
                              axis=1, keepdims=True)
            new = BETA_TWO * old_col + KEEP * (row_sum / n_col)
            row_out[pl.ds(ROW_AT[m] + 16 * h, 16), :] = jnp.broadcast_to(new, (16, 128))
            total = total + jnp.sum(new, axis=0, keepdims=True)
            new_rows.append((new, here, squares))
        mean = total / n_loc
        for new, here, squares in new_rows:
            inv = mean / new
            for u in here:
                c = UNITS[u][2] // 512
                col_s[c] = col_s[c] + jnp.sum(squares[u] + EPS_SQUARE, axis=0, keepdims=True)
                col_d[c] = col_d[c] + jnp.sum(squares[u] * inv, axis=0, keepdims=True)
        for g in range(n_col // 128):
            at = GROUP_AT[m] + g
            part = slice(128 * (g % 4), 128 * (g % 4) + 128)
            row = 0 if at < 32 else 2
            msg[at % 32, row:row + 1, :] = col_s[g // 4][:, part]
            msg[at % 32, row + 1:row + 2, :] = col_d[g // 4][:, part]
        w = weights[m][m] if m < 4 else weights[m][...]
        w_sq = sum_all(w * w)
        scalars = scalars + jnp.where(lane == m, total, 0.0) + jnp.where(lane == 8 + m, w_sq, 0.0)

    @pl.loop(0, 32)
    def _(p):
        msg[p, 4:5, :] = scalars

    def exchange(k, src_of, dst):
        sends = []
        for t in range(1, 32):
            to = (me + t) % 32
            sends.append(pltpu.make_async_remote_copy(
                src_ref=src_of(to), dst_ref=dst.at[me], send_sem=x_sem.at[2 * k], recv_sem=x_sem.at[2 * k + 1],
                device_id=(to,), device_id_type=MESH))
        for send in sends:
            send.start()

    def all_in(k, dst):
        some = dst.at[pl.ds(0, 31)]
        pltpu.make_async_copy(some, some, x_sem.at[2 * k + 1]).wait()

    def all_out(k, dst):
        some = dst.at[pl.ds(0, 31)]
        pltpu.make_async_copy(some, some, x_sem.at[2 * k]).wait()

    exchange(0, lambda to: msg.at[to], rx)
    rx[me] = msg[me]
    all_in(0, rx)

    scal = rx[:, 4, :]
    mat0, mat1 = me // 8, 4 + me // 4
    n_loc1 = jnp.where(me < 4, 32.0, 16.0)
    n_row1 = jnp.where(me < 4, 1024.0, 512.0)
    lanes = lax.broadcasted_iota(jnp.int32, (32, 128), 1)

    def group(row, mat, n_row):
        sums = jnp.sum(jnp.where(lanes == mat, scal, 0.0), axis=1, keepdims=True)
        ratio = jnp.sum(sums, axis=0, keepdims=True) / 32.0 / sums
        s_sum = jnp.sum(rx[:, row, :], axis=0, keepdims=True)
        d_sum = jnp.sum(rx[:, row + 1, :] * ratio, axis=0, keepdims=True)
        at = me + 32 * (row // 2)
        new = BETA_TWO * col_in[pl.ds(at, 1), :] + KEEP * (s_sum / n_row)
        part = jnp.sum(d_sum / new, axis=1, keepdims=True)
        return new, jnp.broadcast_to(part, (1, 128))

    new0, part0 = group(0, mat0, 1024.0)
    new1, part1 = group(2, jnp.minimum(mat1, 5), n_row1)
    tile[...] = jnp.zeros((8, 128), F32)
    tile[0:1, :] = new0
    tile[1:2, :] = new1
    tile[2:3, :] = part0
    tile[3:4, :] = part1
    exchange(1, lambda to: tile, rb)
    rb[me] = tile[...]
    stat_out[pl.ds(32, 1), 0:1, :] = jnp.sum(scal, axis=0, keepdims=True).reshape(1, 1, 128)
    all_in(1, rb)

    @pl.loop(0, 32)
    def _(p):
        stat_out[p] = rb[p]

    all_out(0, msg)
    all_out(1, rb)
    for u in range(N_UNITS):
        for s in range(5):
            copy(u, s).wait_send()


def dense_sums(attn_g, ffin_g, ffout_g, attn_w, ffin_w, ffout_w, attn_r, ffin_r, ffout_r, col_in):
    vmem = pl.BlockSpec(memory_space=pltpu.VMEM)
    hbm = pl.BlockSpec(memory_space=pl.ANY)
    block = (BLK_R, BLK_C)
    return pl.pallas_call(
        dense_kernel,
        out_shape=(jax.ShapeDtypeStruct((N_UNITS,) + block, F32), jax.ShapeDtypeStruct((176, 128), F32),
                   jax.ShapeDtypeStruct((33, 8, 128), F32)),
        in_specs=[hbm] * 3 + [vmem] * 7,
        out_specs=(vmem,) * 3,
        scratch_shapes=[
            pltpu.VMEM((N_UNITS, 32) + block, jnp.bfloat16),
            pltpu.VMEM((N_UNITS, 16) + block, F32),
            pltpu.VMEM((N_UNITS, 16) + block, F32),
            pltpu.VMEM((N_UNITS, 8) + block, F32),
            pltpu.VMEM((N_UNITS, 4) + block, F32),
            pltpu.VMEM((N_UNITS, 2) + block, F32),
            pltpu.VMEM((N_UNITS, 1) + block, F32),
            pltpu.VMEM((32, 8, 128), F32),
            pltpu.VMEM((32, 8, 128), F32),
            pltpu.VMEM((8, 128), F32),
            pltpu.VMEM((32, 8, 128), F32),
            pltpu.SemaphoreType.DMA((N_UNITS,)),
            pltpu.SemaphoreType.DMA((5, N_UNITS)),
            pltpu.SemaphoreType.DMA((5, N_UNITS)),
            pltpu.SemaphoreType.DMA((4,)),
        ],
        compiler_params=pltpu.CompilerParams(has_side_effects=True, vmem_limit_bytes=56 * 2 ** 20),
        name="dense_sums",
    )(attn_g, ffin_g, ffout_g, attn_w, ffin_w, ffout_w, attn_r, ffin_r, ffout_r, col_in)


def factored_step(gradient, weight, row_state, col_state):
    n_rows = gradient.shape[-2]
    n_elems = n_rows * gradient.shape[-1]
    square = gradient * gradient + EPS_SQUARE
    row_new = BETA_TWO * row_state + KEEP * jnp.mean(square, axis=-1)
    col_new = BETA_TWO * col_state + KEEP * (jnp.sum(square, axis=-2) / n_rows)
    row_mean = jnp.sum(row_new, axis=-1) / n_rows
    row_factor = lax.rsqrt(row_new / row_mean[..., None])
    update = gradient * row_factor[..., :, None] * lax.rsqrt(col_new)[..., None, :]
    upd_rms = jnp.sqrt(jnp.sum(update * update, axis=(-2, -1)) / n_elems)
    w_rms = jnp.sqrt(jnp.sum(weight * weight, axis=(-2, -1)) / n_elems)
    step_coeff = LEARN_RATE * jnp.maximum(EPS_SCALE, w_rms) / jnp.maximum(1.0, upd_rms)
    return weight - step_coeff[..., None, None] * update, row_new, col_new


def solution(mesh):
    dense_specs = (
        (P("dp"), P(None, "dp", None), P(None, "dp"), P()),
        (P("dp"), P("dp", None), P("dp"), P()),
        (P("dp"), P("dp", None), P("dp"), P()),
    )
    expert_specs = ((P("dp"), P("dp"), P("dp"), P("dp")),) * 2
    all_specs = dense_specs + expert_specs
    in_specs = tuple(part_spec for group in all_specs for part_spec in group)
    out_specs = tuple(part_spec for group in all_specs for part_spec in group[1:])

    def update_all(*arrays):
        (ag, aw, ar, ac, ig, iw, ir, ic, og, ow, orow, oc) = arrays[:12]
        col_in = jnp.concatenate([ac.reshape(-1, 128), ic.reshape(-1, 128), oc.reshape(-1, 128),
                                  jnp.ones((20, 128), F32)])
        gsum, rows, stat = dense_sums(
            ag.reshape(4, 32, 32, 1024), ig.reshape(32, 32, 512), og.reshape(32, 16, 1024), aw, iw, ow,
            ar, ir.reshape(1, 32), orow.reshape(1, 16), col_in)
        results = []
        scal = stat[32, 0]
        for m in range(6):
            n_row, n_col, n_loc = N_ROWS[m], N_COLS[m], LOC_ROWS[m]
            here = [u for u in range(N_UNITS) if UNITS[u][0] == m]
            g = jnp.concatenate([jnp.concatenate([gsum[u] for u in here if UNITS[u][1] == 16 * h], axis=1)
                                 for h in range(n_loc // 16)], axis=0)
            w = aw[m] if m < 4 else (iw, ow)[m - 4]
            r_new = rows[ROW_AT[m]:ROW_AT[m] + n_loc, 0]
            if m < 4:
                c_new = stat[8 * m:8 * m + 8, 0].reshape(-1)
                part = jnp.sum(stat[8 * m:8 * m + 8, 2, 0])
            elif m == 4:
                c_new = stat[0:4, 1].reshape(-1)
                part = jnp.sum(stat[0:4, 3, 0])
            else:
                c_new = stat[4:12, 1].reshape(-1)
                part = jnp.sum(stat[4:12, 3, 0])
            n_elems = n_row * n_col
            factor = lax.rsqrt(r_new / (scal[m] / n_row))
            upd_rms = jnp.sqrt(part / n_elems)
            w_rms = jnp.sqrt(scal[8 + m] / n_elems)
            coeff = LEARN_RATE * jnp.maximum(EPS_SCALE, w_rms) / jnp.maximum(1.0, upd_rms)
            results.append((w - coeff * (g * factor[:, None] * lax.rsqrt(c_new)[None, :]), r_new, c_new))
        out = [jnp.stack([results[m][k] for m in range(4)]) for k in range(3)]
        out += list(results[4]) + list(results[5])
        for index in (3, 4):
            out.extend(factored_step(*arrays[4 * index: 4 * index + 4]))
        return tuple(out)

    return jax.shard_map(update_all, mesh=mesh, in_specs=in_specs, out_specs=out_specs, check_vma=False)
```

time: 577 us -> 165 us (0.29)
  waiting for transfers between devices: 419 us -> 0 us
  Pallas kernels: 0 us -> 112 us
  blocking collectives: 81.5 us -> 0 us
  other arithmetic: 50.5 us -> 26.5 us
    reduce_scatter x3 -> x0, waiting for transfers between devices: 418 us -> none  [update_all(): lax.psum_scatter(grad_local[0].astype(jnp.float32), 'dp', scatter_dimensi...]
    pallas_call x0 -> x1, Pallas kernels: none -> 112 us  [dense_sums(): pl.pallas_call(dense_kernel, out_shape=(jax.ShapeDtypeStruct((N_UNITS,) +...]
    psum x2 -> x0, blocking collectives: 81.5 us -> none  [dp_total(): return lax.psum(value, 'dp') if across else value]
    convert_element_type x3 -> x0, other arithmetic: 15.8 us -> none  [update_all(): grad_local[0].astype(jnp.float32)]
    reduce_sum x19 -> x9, other arithmetic: 21.9 us -> 14.6 us  [the longest x2 5.62 us: factored_step(): w_rms = jnp.sqrt(jnp.sum(weight * weight, axis=(-2, -1)) / n_elems)]
    sub x5 -> x2, other arithmetic: 9.68 us -> 3.4 us  [factored_step(): return (weight - step_coeff[..., None, None] * update, row_new, col_new)]
  transfers between devices with their start and end apart: 3 -> 0, of which waited for: 3 -> 0; matrix products, arithmetic and copies ran while one was open for 6% -> 0% of each run, Pallas kernels for 0% -> 0%
where the time goes in v1:
time: 165 us; the launch traced here: 164 us
  Pallas kernels  112 us (68%)
  other arithmetic  26.5 us (16%)
  between operations  17.5 us (11%)
  local copies, waits for them, and re-layouts  7.73 us (5%)
    pallas_call x1, Pallas kernels, dense_sums(): pl.pallas_call(dense_kernel, out_shape=(jax.ShapeDtypeStruct((N_UNITS,) +...  112 us
    reduce_sum x2, other arithmetic, factored_step(): w_rms = jnp.sqrt(jnp.sum(weight * weight, axis=(-2, -1)) / n_elems)  5.62 us
    reduce_sum x2, other arithmetic, factored_step(): upd_rms = jnp.sqrt(jnp.sum(update * update, axis=(-2, -1)) / n_elems)  4.13 us
    sub x2, other arithmetic, factored_step(): return (weight - step_coeff[..., None, None] * update, row_new, col_new)  3.4 us

profile of v1, /device:TPU:0, one launch (start us, length us, event | category | flops | bytes accessed | tf_op | source)
XLA Modules:
  0.0 164.1 jit_solution(18107769217287101344)
XLA Ops:
  0.7 2.9 %multiply_reduce_fusion.1 = f32[]{:T(128)} fusion(f32[1,512,1024]{2,1,0:T(8,128)} %param.37), kind=kLoop, calls=%fused_computation.4 | loop fusion | flops 1048575 | bytes 2097156 | tf_op jit(solution)/shard_map/reduce_sum | solution.py:259
  4.2 2.7 %multiply_reduce_fusion.3 = f32[]{:T(128)} fusion(f32[1,1024,512]{2,1,0:T(8,128)} %param.33), kind=kLoop, calls=%fused_computation.9 | loop fusion | flops 1048575 | bytes 2097156 | tf_op jit(solution)/shard_map/reduce_sum | solution.py:259
  7.7 0.1 pad.43.clone
  7.8 0.4 fusion.1
  8.2 1.1 copy-done.1
  9.3 0.4 fusion.3
  9.7 1.2 fusion.22
  11.6 1.2 fusion.23
  13.5 2.9 %multiply_reduce_fusion = f32[]{:T(128)} fusion(f32[1,512,1024]{2,1,0:T(8,128)} %param.36, f32[1024]{0:T(1024)S(1)} %bitcast.104, f32[512]{0:T(512)S(1)} %bitcast.108), kind=kLoop, calls=%fused_computation.1 | loop fusion | flops 2097151 | bytes 2103300 | tf_op jit(solution)/shard_map/reduce_sum | solution.py:258
  17.1 1.3 multiply_reduce_fusion.2
  19.2 0.7 maximum_maximum_fusion.col_in
  19.9 112.3 %dense_sums.1 = (f32[20,16,512]{2,1,0:T(8,128)}, f32[176,128]{1,0:T(8,128)}, f32[33,8,128]{2,1,0:T(8,128)}) custom-call(bf16[4,32,32,1024]{3,2,1,0:T(8,128)(2,1)} %bitcast.101, bf16[32,32,512]{2,1,0:T(8,128)(2,1)} %bitcast.102, bf16[32,16,1024]{2,1,0:T(8,128)(2,1)} %bitcast.103, f32[4,32,1024]{2,1,0:T(8,128)} %attn_w.1, f32[32,512]{1,0:T(8,128)} %ffin_w.1, ...), custom_call_target="tpu_custom_call" | custom-call | tf_op jit(solution)/shard_map/dense_sums/pallas_call | solution.py:221
  132.2 1.4 slice_reduce_fusion.11
  134.2 0.7 slice.233
  135.0 1.5 slice_reduce_fusion.6
  139.9 1.8 %fusion.26 = (f32[1,1,1]{2,1,0:T(1,128)}, f32[1,1,1]{2,1,0:T(1,128)}, f32[1,1,1]{2,1,0:T(1,128)}, f32[1,1,1]{2,1,0:T(1,128)}, f32[1,1,1]{2,1,0:T(1,128)}, /*inde...) fusion(f32[33,8,128]{2,1,0:T(8,128)} %get-tuple-element.18), kind=kLoop, calls=%fused_computation.110 | loop fusion | bytes 96 | tf_op jit(solution)/shard_map/slice | solution.py:303
  150.0 0.9 fusion.27
  150.9 1.3 slice_reduce_fusion.5
  152.2 1.5 slice_reduce_fusion
  153.7 0.6 pad_maximum_fusion.2
  154.3 0.6 pad_maximum_fusion.1
  154.9 0.8 slice_bitcast_fusion.19
  155.7 1.1 slice_bitcast_fusion.1
  156.8 0.7 fusion.21
  157.5 0.7 fusion.18
  158.3 0.1 fusion.12
  158.4 0.1 fusion.6
  158.6 0.8 pad_maximum_fusion
  159.4 1.7 %multiply_subtract_fusion.1 = f32[1,1024,512]{2,1,0:T(8,128)} fusion(f32[1,1024,512]{2,1,0:T(8,128)S(1)} %copy-done.3, f32[1,1024,512]{2,1,0:T(8,128)S(1)} %copy-done, f32[]{:T(128)S(6)} %div.224, f32[512]{0:T(512)S(1)} %bitcast.111, f32[1024]{0:T(1024)S(1)} %bitcast.107), kind=kLoop, calls=%fused_computation.5 | loop fusion | flops 2097152 | bytes 6297604 | tf_op jit(solution)/shard_map/sub | solution.py:261
  161.1 0.4 copy-done.2
  161.5 0.8 copy-done.4
  162.4 1.7 %multiply_subtract_fusion = f32[1,512,1024]{2,1,0:T(8,128)} fusion(f32[1,512,1024]{2,1,0:T(8,128)S(1)} %copy-done.4, f32[1,512,1024]{2,1,0:T(8,128)S(1)} %copy-done.2, f32[]{:T(128)S(6)} %div.225, f32[1024]{0:T(1024)S(1)} %bitcast.105, f32[512]{0:T(512)S(1)} %bitcast.109), kind=kLoop, calls=%fused_computation | loop fusion | flops 2097152 | bytes 6297604 | tf_op jit(solution)/shard_map/sub | solution.py:261
  (49 shorter events, 0.2 us)
Async XLA Ops:
  0.6 7.1 %copy-start = (f32[1,1024,512]{2,1,0:T(8,128)S(1)}, f32[1,1024,512]{2,1,0:T(8,128)}, u32[]{:S(2)}) copy-start(f32[1,1024,512]{2,1,0:T(8,128)} %param.32) | copy-start | bytes 6291460
  7.7 1.6 copy-start.1
  7.8 1.9 %copy-start.17 = (f32[1,512]{1,0:T(1,128)S(1)}, f32[1,512]{1,0:T(1,128)}, u32[]{:S(2)}) copy-start(f32[1,512]{1,0:T(1,128)} %param.38) | copy-start | bytes 6148
  7.8 1.9 %copy-start.18 = (f32[1,512]{1,0:T(1,128)S(1)}, f32[1,512]{1,0:T(1,128)}, u32[]{:S(2)}) copy-start(f32[1,512]{1,0:T(1,128)} %param.35) | copy-start | bytes 6148
  7.8 3.8 %copy-start.13 = (f32[1,1024]{1,0:T(1,128)S(1)}, f32[1,1024]{1,0:T(1,128)}, u32[]{:S(2)}) copy-start(f32[1,1024]{1,0:T(1,128)} %param.39) | copy-start | bytes 12292
  7.8 3.8 %copy-start.14 = (f32[1,1024]{1,0:T(1,128)S(1)}, f32[1,1024]{1,0:T(1,128)}, u32[]{:S(2)}) copy-start(f32[1,1024]{1,0:T(1,128)} %param.34) | copy-start | bytes 12292
  10.9 7.5 %copy-start.12 = (f32[1,512]{1,0:T(1,128)}, f32[1,512]{1,0:T(1,128)S(1)}, u32[]{:S(2)}) copy-start(f32[1,512]{1,0:T(1,128)S(1)} %get-tuple-element.43) | copy-start | bytes 6148
  12.8 5.6 %copy-start.9 = (f32[1,1024]{1,0:T(1,128)}, f32[1,1024]{1,0:T(1,128)S(1)}, u32[]{:S(2)}) copy-start(f32[1,1024]{1,0:T(1,128)S(1)} %get-tuple-element.104) | copy-start | bytes 12292
  13.5 5.7 %copy-start.10 = (f32[4,1024]{1,0:T(4,128)S(1)}, f32[4,1024]{1,0:T(4,128)}, u32[]{:S(2)}) copy-start(f32[4,1024]{1,0:T(4,128)} %param.23) | copy-start | bytes 49156
  13.5 5.7 %copy-start.15 = (f32[1024]{0:T(1024)S(1)}, f32[1024]{0:T(1024)}, u32[]{:S(2)}) copy-start(f32[1024]{0:T(1024)} %param.31) | copy-start | bytes 12292
  13.5 5.7 %copy-start.16 = (f32[512]{0:T(512)S(1)}, f32[512]{0:T(512)}, u32[]{:S(2)}) copy-start(f32[512]{0:T(512)} %param.27) | copy-start | bytes 6148
  19.9 136.9 %copy-start.6 = (f32[16,1024]{1,0:T(8,128)S(1)}, f32[16,1024]{1,0:T(8,128)}, u32[]{:S(2)}) copy-start(f32[16,1024]{1,0:T(8,128)} %ffout_w.1) | copy-start | bytes 196612
  19.9 137.6 %copy-start.7 = (f32[32,512]{1,0:T(8,128)S(1)}, f32[32,512]{1,0:T(8,128)}, u32[]{:S(2)}) copy-start(f32[32,512]{1,0:T(8,128)} %ffin_w.1) | copy-start | bytes 196612
  132.2 26.1 %copy-start.5 = (f32[4,32,1024]{2,1,0:T(8,128)S(1)}, f32[4,32,1024]{2,1,0:T(8,128)}, u32[]{:S(2)}) copy-start(f32[4,32,1024]{2,1,0:T(8,128)} %attn_w.1) | copy-start | bytes 1572868
  135.0 23.6 %copy-start.11 = (f32[4,1,128]{2,1,0:T(1,128)}, f32[4,1,128]{2,1,0:T(1,128)S(1)}, u32[]{:S(2)}) copy-start(f32[4,1,128]{2,1,0:T(1,128)S(1)} %slice.233) | copy-start | bytes 6148
  150.9 7.7 %copy-start.8 = (f32[8,1,128]{2,1,0:T(1,128)}, f32[8,1,128]{2,1,0:T(1,128)S(1)}, u32[]{:S(2)}) copy-start(f32[8,1,128]{2,1,0:T(1,128)S(1)} %get-tuple-element.84) | copy-start | bytes 12292
  156.8 2.6 %copy-start.3 = (f32[1,1024,512]{2,1,0:T(8,128)S(1)}, f32[1,1024,512]{2,1,0:T(8,128)}, u32[]{:S(2)}) copy-start(f32[1,1024,512]{2,1,0:T(8,128)} %param.33) | copy-start | bytes 6291460
  159.4 2.1 %copy-start.2 = (f32[1,512,1024]{2,1,0:T(8,128)S(1)}, f32[1,512,1024]{2,1,0:T(8,128)}, u32[]{:S(2)}) copy-start(f32[1,512,1024]{2,1,0:T(8,128)} %param.36) | copy-start | bytes 6291460
  159.4 3.0 %copy-start.4 = (f32[1,512,1024]{2,1,0:T(8,128)S(1)}, f32[1,512,1024]{2,1,0:T(8,128)}, u32[]{:S(2)}) copy-start(f32[1,512,1024]{2,1,0:T(8,128)} %param.37) | copy-start | bytes 6291460

commit v2 on v1

v2 whole, which is shorter than its diff:
```python
import functools

import jax
import jax.numpy as jnp
from jax import lax
from jax.experimental import pallas as pl
from jax.experimental.pallas import tpu as pltpu
from jax.sharding import PartitionSpec as P

D_MODEL, D_FF, LANES, N_DEV = 1024, 512, 128, 32
OPT_STEP = 10
LEARN_RATE = 0.1
EPS_SQUARE = 1e-30
EPS_SCALE = 1e-3
BETA_TWO = 1.0 - OPT_STEP ** -0.8
KEEP = 1.0 - BETA_TWO
F32 = jnp.float32
BLK_R, BLK_C = 16, D_FF
N_UNITS = 20
BIT = {"x": 1, "y": 2, "a": 3, "b": 4}

ORDERS = ("xayb", "yaxb") * 10
STEP_UNITS = "".join((
    "ABCADBEFGHIJCKDLMANOPQBERFSTCDBAGCEHFADBIEGAJCBHFDCKGILEDJHF",
    "EMIKNGFLJHGOKMPIHNLJIQMORKJPNLKMSOQTLMRPNOQSNROTPQSRPTQSRTST",
))
STEPS = [(ord(u) - ord("A"), STEP_UNITS[:n].count(u)) for n, u in enumerate(STEP_UNITS)]

UNITS = [(m, 16 * r, D_FF * c) for m in range(4) for r in range(2) for c in range(2)]
UNITS += [(4, 0, 0), (4, 16, 0), (5, 0, 0), (5, 0, D_FF)]
N_ROWS = (D_MODEL, D_MODEL, D_MODEL, D_MODEL, D_MODEL, D_FF)
N_COLS = (D_MODEL, D_MODEL, D_MODEL, D_MODEL, D_FF, D_MODEL)
LOC_ROWS = (N_DEV, N_DEV, N_DEV, N_DEV, N_DEV, 16)
ROW_AT = (0, N_DEV, 64, 96, LANES, 160)
GROUP_AT = (0, 8, 16, 24, N_DEV, 36)
EARLY = 4
WORK_AT, WORK_EVERY = 16, 3
MESH = pl.DeviceIdType.MESH


def sum_of(value, axis):
    return jnp.sum(value, axis=axis, keepdims=True)


over_rows, over_cols = (functools.partial(sum_of, axis=axis) for axis in range(2))


def sum_all(value):
    return over_rows(over_cols(value))


def step_size(upd_sq, w_sq, n_elems):
    w_rms = jnp.sqrt(w_sq / n_elems)
    return LEARN_RATE * jnp.maximum(EPS_SCALE, w_rms) / jnp.maximum(1.0, jnp.sqrt(upd_sq / n_elems))


def expert_work(loads, arrays, results, sums, factor, acc, out_sem, outs):
    g_v, w_v = arrays[0].at[0], arrays[1].at[0]
    r_old, c_old = arrays[2:]
    w_new, r_new, c_new = results
    n_rows, n_cols = g_v.shape
    c_acc, w_acc, u_acc = (acc.at[n, :, pl.ds(0, n_cols)] for n in range(3))
    quarter = n_rows // 4

    def begin():
        for load in loads:
            load.wait()
        for ref in (c_acc, w_acc, u_acc):
            ref[...] = jnp.zeros((8, n_cols), F32)

    def squares(b):
        c_sum, w_sum = c_acc[...], w_acc[...]
        for r in range(16):
            at = slice(LANES * b + 8 * r, LANES * b + 8 * r + 8)
            sq = g_v[at, :] * g_v[at, :] + EPS_SQUARE
            c_sum = c_sum + sq
            w_sum = w_sum + w_v[at, :] * w_v[at, :]
            sums[8 * r:8 * r + 8, :] = jnp.broadcast_to(over_cols(sq), (8, LANES))
        c_acc[...], w_acc[...] = c_sum, w_sum
        part = slice(LANES * b, LANES * b + LANES)
        r_new[:, part] = BETA_TWO * r_old[:, part] + KEEP * (jnp.transpose(sums[...])[0:1, :] / n_cols)

    def factors():
        c_new[...] = BETA_TWO * c_old[...] + KEEP * (over_rows(c_acc[...]) / n_rows)
        mean = over_cols(r_new[...]) / n_rows
        row_factor = lax.rsqrt(r_new[...] / mean)
        for b in range(n_rows // LANES):
            part = slice(LANES * b, LANES * b + LANES)
            factor[part, :] = jnp.transpose(jnp.broadcast_to(row_factor[:, part], (LANES, LANES)))

    def update(q):
        col_factor = lax.rsqrt(c_new[...])

        @pl.loop(0, quarter // N_DEV)
        def _(n):
            at = pl.ds(q * quarter + n * N_DEV, N_DEV)
            upd = g_v[at, :] * factor[at, 0:1] * col_factor
            g_v[at, :] = upd
            sq = upd * upd
            u_acc[...] = u_acc[...] + sq[0:8] + sq[8:16] + sq[16:24] + sq[24:N_DEV]

    def finish(q):
        coeff = step_size(sum_all(u_acc[...]), sum_all(w_acc[...]), n_rows * n_cols)

        @pl.loop(0, quarter // N_DEV)
        def _(n):
            at = pl.ds(q * quarter + n * N_DEV, N_DEV)
            w_v[at, :] = w_v[at, :] - coeff * g_v[at, :]

        part = pl.ds(q * quarter, quarter)
        outs.append(pltpu.make_async_copy(w_v.at[part], w_new.at[part], out_sem(q)))
        outs[-1].start()

    pieces = [begin] + [functools.partial(squares, b) for b in range(n_rows // LANES)] + [factors]
    return pieces + [functools.partial(f, q) for f in (update, finish) for q in range(4)]


def dense_kernel(attn_g, ffin_g, ffout_g, *refs):
    small, expert_in, refs = refs[:9], refs[9:17], refs[17:]
    (gsum, row_out, stat_out), expert_out, scratch = refs[:3], refs[3:9], refs[9:]
    small_vmem, expert_v, scratch = scratch[:9], scratch[9:17], scratch[17:]
    raw, stage, r0, r1, r2, r3, r4, msg, rx, tile, rb, *scratch = scratch
    sums, factor, acc, ld_sem, s_sem, r_sem, x_sem, e_sem = scratch
    attn_w, ffin_w, ffout_w, attn_r, ffin_r, ffout_r, attn_c, ffin_c, ffout_c = small_vmem
    me = lax.axis_index("dp")
    bits = [(me // 2 ** k) % 2 for k in range(5)]
    partner = [me + (1 - 2 * bits[k]) * 2 ** k for k in range(5)]
    core = bits[0]
    recvs = (r0, r1, r2, r3, r4)

    def source(u):
        m, row, col = UNITS[u]
        if m < 4:
            return attn_g.at[m, :, pl.ds(row, BLK_R), pl.ds(col, BLK_C)]
        ref = ffin_g if m == 4 else ffout_g
        return ref.at[:, pl.ds(row, BLK_R), pl.ds(col, BLK_C)]

    barrier = pltpu.get_barrier_semaphore()
    for t in range(1, N_DEV):
        pl.semaphore_signal(barrier, inc=1, device_id=((me + t) % N_DEV,), device_id_type=MESH)
    loads = [pltpu.make_async_copy(source(u), raw.at[u], ld_sem.at[u]) for u in range(N_UNITS)]
    for load in loads:
        load.start()
    small_loads = [pltpu.make_async_copy(a, b, ld_sem.at[N_UNITS]) for a, b in zip(small, small_vmem)]
    for load in small_loads:
        load.start()

    def dest(order, i):
        return sum(((i // 2 ** (3 - j)) % 2) * 2 ** BIT[order[j]] for j in range(4))

    def copy(u, s):
        order = ORDERS[u]
        if s == 0:
            src, to = stage.at[u], partner[0]
        else:
            keep = sum(bits[BIT[order[j]]] * 2 ** (3 - j) for j in range(s - 1))
            k = BIT[order[s - 1]]
            src = r0.at[u, pl.ds(keep + (1 - bits[k]) * 2 ** (4 - s), 2 ** (4 - s))]
            to = partner[k]
        return pltpu.make_async_remote_copy(
            src_ref=src, dst_ref=recvs[s].at[u], send_sem=s_sem.at[s, u], recv_sem=r_sem.at[s, u],
            device_id=(to,), device_id_type=MESH)

    def block_sum(u, s, i, d):
        total = raw[u, d].astype(F32)
        for j in range(s):
            total = total + recvs[j][u, i % 2 ** (4 - j)]
        return total

    def to_f32(u):
        loads[u].wait()

        @pl.loop(0, 16)
        def _(i):
            stage[u, i] = raw[u, dest(ORDERS[u], i) + 1 - core].astype(F32)

    def step(u, s):
        order = ORDERS[u]
        if s == 0:
            to_f32(u)
        else:
            copy(u, s - 1).wait_recv()
            base = sum(bits[BIT[order[j]]] * 2 ** (3 - j) for j in range(min(s - 1, 4)))
            if s == 5:
                gsum[u] = block_sum(u, 5, base, me) * (1.0 / 32.0)
                return
            base = base + (1 - bits[BIT[order[s - 1]]]) * 2 ** (4 - s)

            @pl.loop(0, 2 ** (4 - s))
            def _(n):
                i = base + n
                r0[u, i] = block_sum(u, s, i, dest(order, i) + core)
        copy(u, s).start()

    stage_zero = [u for u, s in STEPS if s == 0]
    for u in stage_zero[:EARLY]:
        to_f32(u)
    pl.semaphore_wait(barrier, 31)
    for u in stage_zero[:EARLY]:
        copy(u, 0).start()
    expert_loads = [pltpu.make_async_copy(a, b, e_sem.at[n]) for n, (a, b) in enumerate(zip(expert_in, expert_v))]
    work = []
    outs = []
    for k in range(2):
        half = slice(4 * k, 4 * k + 4)
        work += expert_work(expert_loads[half], expert_v[half], expert_out[3 * k:3 * k + 3], sums, factor,
                            acc.at[k], lambda n, k=k: e_sem.at[8 + 4 * k + n], outs)
    for n, (u, s) in enumerate(STEPS):
        if n == WORK_AT - 4:
            for load in expert_loads:
                load.start()
        if s > 0 or u not in stage_zero[:EARLY]:
            step(u, s)
        if n >= WORK_AT and n % WORK_EVERY == 0 and work:
            work.pop(0)()
    for piece in work:
        piece()

    for load in small_loads:
        load.wait()

    rows_in = (attn_r, attn_r, attn_r, attn_r, ffin_r, ffout_r)
    weights = (attn_w, attn_w, attn_w, attn_w, ffin_w, ffout_w)
    lane = lax.broadcasted_iota(jnp.int32, (1, LANES), 1)
    scalars = jnp.zeros((1, LANES), F32)
    msg[...] = jnp.zeros((N_DEV, 8, LANES), F32)
    for m in range(6):
        units = [u for u in range(N_UNITS) if UNITS[u][0] == m]
        n_loc, n_col = LOC_ROWS[m], N_COLS[m]
        col_s = [0.0] * (n_col // D_FF)
        col_d = [0.0] * (n_col // D_FF)
        new_rows = []
        total = jnp.zeros((1, 1), F32)
        for h in range(n_loc // 16):
            here = [u for u in units if UNITS[u][1] == 16 * h]
            squares = {u: gsum[u] * gsum[u] for u in here}
            row_sum = sum(over_cols(squares[u] + EPS_SQUARE) for u in here)
            old = rows_in[m][m, :] if m < 4 else rows_in[m][0, :]
            pick = lax.broadcasted_iota(jnp.int32, (16, n_loc), 0) + 16 * h == lax.broadcasted_iota(
                jnp.int32, (16, n_loc), 1)
            old_col = over_cols(jnp.where(pick, jnp.broadcast_to(old.reshape(1, n_loc), (16, n_loc)), 0.0))
            new = BETA_TWO * old_col + KEEP * (row_sum / n_col)
            row_out[pl.ds(ROW_AT[m] + 16 * h, 16), :] = jnp.broadcast_to(new, (16, LANES))
            total = total + over_rows(new)
            new_rows.append((new, here, squares))
        mean = total / n_loc
        for new, here, squares in new_rows:
            inv = mean / new
            for u in here:
                c = UNITS[u][2] // D_FF
                col_s[c] = col_s[c] + over_rows(squares[u] + EPS_SQUARE)
                col_d[c] = col_d[c] + over_rows(squares[u] * inv)
        for g in range(n_col // LANES):
            at = GROUP_AT[m] + g
            part = slice(LANES * (g % 4), LANES * (g % 4) + LANES)
            row = 0 if at < N_DEV else 2
            msg[at % N_DEV, row:row + 1, :] = col_s[g // 4][:, part]
            msg[at % N_DEV, row + 1:row + 2, :] = col_d[g // 4][:, part]
        w = weights[m][m] if m < 4 else weights[m][...]
        w_sq = sum_all(w * w)
        scalars = scalars + jnp.where(lane == m, total, 0.0) + jnp.where(lane == 8 + m, w_sq, 0.0)

    @pl.loop(0, N_DEV)
    def _(p):
        msg[p, 4:5, :] = scalars

    def exchange(k, src_of, dst):
        sends = []
        for t in range(1, N_DEV):
            to = (me + t) % N_DEV
            sends.append(pltpu.make_async_remote_copy(
                src_ref=src_of(to), dst_ref=dst.at[me], send_sem=x_sem.at[2 * k], recv_sem=x_sem.at[2 * k + 1],
                device_id=(to,), device_id_type=MESH))
        for send in sends:
            send.start()

    def all_in(k, dst):
        some = dst.at[pl.ds(0, 31)]
        pltpu.make_async_copy(some, some, x_sem.at[2 * k + 1]).wait()

    def all_out(k, dst):
        some = dst.at[pl.ds(0, 31)]
        pltpu.make_async_copy(some, some, x_sem.at[2 * k]).wait()

    exchange(0, lambda to: msg.at[to], rx)
    rx[me] = msg[me]
    all_in(0, rx)

    scal = rx[:, 4, :]
    mat0, mat1 = me // 8, 4 + me // 4
    n_loc1 = jnp.where(me < 4, 32.0, 16.0)
    n_row1 = jnp.where(me < 4, 1024.0, 512.0)
    lanes = lax.broadcasted_iota(jnp.int32, (N_DEV, LANES), 1)

    def group(row, mat, n_row, old):
        sums = over_cols(jnp.where(lanes == mat, scal, 0.0))
        ratio = over_rows(sums) / 32.0 / sums
        s_sum = over_rows(rx[:, row, :])
        d_sum = over_rows(rx[:, row + 1, :] * ratio)
        new = BETA_TWO * old + KEEP * (s_sum / n_row)
        part = over_cols(d_sum / new)
        return new, jnp.broadcast_to(part, (1, LANES))

    def lanes_at(k):
        return pl.ds(pl.multiple_of(k * LANES, LANES), LANES)

    old0 = sum(jnp.where(mat0 == m, attn_c[m:m + 1, lanes_at(me % 8)], 0.0) for m in range(4))
    old1 = jnp.where(me < 4, ffin_c[:, lanes_at(me % 4)], ffout_c[:, lanes_at((me + 4) % 8)])
    new0, part0 = group(0, mat0, 1024.0, old0)
    new1, part1 = group(2, jnp.minimum(mat1, 5), n_row1, old1)
    tile[...] = jnp.zeros((8, LANES), F32)
    tile[0:1, :] = new0
    tile[1:2, :] = new1
    tile[2:3, :] = part0
    tile[3:4, :] = part1
    exchange(1, lambda to: tile, rb)
    rb[me] = tile[...]
    stat_out[pl.ds(N_DEV, 1), 0:1, :] = over_rows(scal).reshape(1, 1, LANES)
    all_in(1, rb)

    @pl.loop(0, N_DEV)
    def _(p):
        stat_out[p] = rb[p]

    for out in outs:
        out.wait()
    all_out(0, msg)
    all_out(1, rb)
    for u in range(N_UNITS):
        for s in range(5):
            copy(u, s).wait_send()


ANY = pl.BlockSpec(memory_space=pl.ANY)
VMEM = pl.BlockSpec(memory_space=pltpu.VMEM)


EXPERT_SHAPES = ((D_MODEL, D_FF), (1, D_MODEL), (1, D_FF), (D_FF, D_MODEL), (1, D_FF), (1, D_MODEL))


def shapes_of(*shapes):
    return tuple(jax.ShapeDtypeStruct(shape, F32) for shape in shapes)


def dense_sums(grads, small, experts):
    block = (BLK_R, BLK_C)
    halves = [pltpu.VMEM((N_UNITS, 2 ** k) + block, F32) for k in (4, 4, 3, 2, 1, 0)]
    return pl.pallas_call(
        dense_kernel,
        out_shape=shapes_of((N_UNITS,) + block, (176, LANES), (33, 8, LANES), *EXPERT_SHAPES),
        in_specs=[ANY] * 20,
        out_specs=(VMEM,) * 3 + (ANY, VMEM, VMEM) * 2,
        scratch_shapes=[pltpu.VMEM(a.shape, F32) for a in small + experts] + [
            pltpu.VMEM((N_UNITS, N_DEV) + block, jnp.bfloat16), *halves,
            pltpu.VMEM((N_DEV, 8, LANES), F32), pltpu.VMEM((N_DEV, 8, LANES), F32),
            pltpu.VMEM((8, LANES), F32), pltpu.VMEM((N_DEV, 8, LANES), F32),
            pltpu.VMEM((LANES, LANES), F32), pltpu.VMEM((D_MODEL, LANES), F32), pltpu.VMEM((2, 3, 8, D_MODEL), F32),
            pltpu.SemaphoreType.DMA((N_UNITS + 1,)),
            pltpu.SemaphoreType.DMA((5, N_UNITS)),
            pltpu.SemaphoreType.DMA((5, N_UNITS)),
            pltpu.SemaphoreType.DMA((4,)),
            pltpu.SemaphoreType.DMA((16,)),
        ],
        compiler_params=pltpu.CompilerParams(
            has_side_effects=True, vmem_limit_bytes=58 * 2 ** 20, collective_id=1),
        name="dense_sums",
    )(*grads, *small, *experts)


def final_kernel(gsum, rows, stat, *refs):
    dense_w, expert_in, refs = refs[:3], refs[3:9], refs[9:]
    (aw_new, ar_new, ac_new, iw_new, ir_new, ic_new, ow_new, or_new, oc_new), refs = refs[:9], refs[9:]
    expert_out, (gs_v, aw, iw, ow, e_in, e_out, in_sem, out_sem) = refs[:6], refs[6:]

    dense_loads = [pltpu.make_async_copy(a, b, in_sem.at[n])
                   for n, (a, b) in enumerate(zip((gsum,) + dense_w, (gs_v, aw, iw, ow)))]
    moves = []
    for k, buffer in enumerate((e_in, e_out)):
        n_rows = buffer.shape[0] // 4
        for q in range(4):
            part = pl.ds(q * n_rows, n_rows)
            moves.append((pltpu.make_async_copy(expert_in[3 * k].at[part], buffer.at[part], in_sem.at[4 + 4 * k + q]),
                          pltpu.make_async_copy(buffer.at[part], expert_out[3 * k].at[0, part],
                                                out_sem.at[3 + 4 * k + q])))
    for load in dense_loads:
        load.start()
    for load, _ in moves:
        load.start()
    for k in (1, 2, 4, 5):
        expert_out[k][...] = expert_in[k][...]
    for load in dense_loads:
        load.wait()

    scal = stat[N_DEV, 0:1, :]
    lane = lax.broadcasted_iota(jnp.int32, (1, LANES), 1)
    flipped = (jnp.transpose(rows[0:LANES, :]), jnp.transpose(rows[48:176, :]))
    for m in range(4):
        ar_new[m:m + 1, :] = flipped[0][0:1, N_DEV * m:N_DEV * m + N_DEV]
    ir_new[...] = flipped[1][0:1, 80:112]
    or_new[...] = flipped[1][0:1, 112:LANES]
    outs = []
    for m in range(6):
        row = 0 if m < 4 else 1
        at = GROUP_AT[m] % N_DEV
        n_groups = N_COLS[m] // LANES
        c_new = jnp.concatenate([stat[at + g, row:row + 1, :] for g in range(n_groups)], axis=1)
        parts = sum(stat[at + g, row + 2:row + 3, 0:1] for g in range(n_groups))
        if m < 4:
            ac_new[m:m + 1, :] = c_new
        else:
            (ic_new, oc_new)[m - 4][...] = c_new
        row_total = over_cols(jnp.where(lane == m, scal, 0.0))
        w_sq = over_cols(jnp.where(lane == 8 + m, scal, 0.0))
        coeff = step_size(parts, w_sq, N_ROWS[m] * N_COLS[m])
        col_factor = lax.rsqrt(c_new)
        w = aw.at[m] if m < 4 else (iw, ow)[m - 4]
        for u in range(N_UNITS):
            if UNITS[u][0] != m:
                continue
            r_at, c_at = UNITS[u][1:]
            r_factor = lax.rsqrt(rows[ROW_AT[m] + r_at:ROW_AT[m] + r_at + BLK_R, 0:1] / (row_total / N_ROWS[m]))
            step = coeff * (gs_v[u] * r_factor * col_factor[:, c_at:c_at + BLK_C])
            part = (slice(r_at, r_at + BLK_R), slice(c_at, c_at + BLK_C))
            w[part] = w[part] - step
        if m >= 3:
            outs.append(pltpu.make_async_copy((aw, iw, ow)[m - 3], (aw_new, iw_new, ow_new)[m - 3],
                                              out_sem.at[m - 3]))
            outs[-1].start()
    for load, out in moves:
        load.wait()
        out.start()
        outs.append(out)
    for out in outs:
        out.wait()


def final_update(sums, dense_w):
    experts = [(1,) + shape if shape[0] > 1 else shape for shape in EXPERT_SHAPES]
    return pl.pallas_call(
        final_kernel,
        out_shape=shapes_of((4, N_DEV, D_MODEL), (4, N_DEV), (4, D_MODEL), (N_DEV, D_FF), (1, N_DEV), (1, D_FF), (16, D_MODEL), (1, 16),
                            (1, D_MODEL), *experts),
        in_specs=[ANY, VMEM, VMEM] + [ANY] * 3 + [ANY, VMEM, VMEM] * 2,
        out_specs=[ANY, VMEM, VMEM] * 5,
        scratch_shapes=[
            pltpu.VMEM((N_UNITS, BLK_R, BLK_C), F32), *[pltpu.VMEM(a.shape, F32) for a in dense_w],
            pltpu.VMEM((D_MODEL, D_FF), F32), pltpu.VMEM((D_FF, D_MODEL), F32),
            pltpu.SemaphoreType.DMA((12,)), pltpu.SemaphoreType.DMA((11,)),
        ],
        compiler_params=pltpu.CompilerParams(vmem_limit_bytes=67043328),
        name="final_update",
    )(*sums[:3], *dense_w, *sums[3:])


def solution(mesh):
    dense_specs = (
        (P("dp"), P(None, "dp", None), P(None, "dp"), P()),
        (P("dp"), P("dp", None), P("dp"), P()),
        (P("dp"), P("dp", None), P("dp"), P()),
    )
    expert_specs = ((P("dp"), P("dp"), P("dp"), P("dp")),) * 2
    all_specs = dense_specs + expert_specs
    in_specs = tuple(part_spec for group in all_specs for part_spec in group)
    out_specs = tuple(part_spec for group in all_specs for part_spec in group[1:])

    def update_all(*arrays):
        (ag, aw, ar, ac, ig, iw, ir, ic, og, ow, orow, oc) = arrays[:12]
        grads = (ag.reshape(4, N_DEV, N_DEV, D_MODEL), ig.reshape(N_DEV, N_DEV, D_FF), og.reshape(N_DEV, 16, D_MODEL))
        sums = dense_sums(grads, (aw, iw, ow, ar, ir.reshape(1, N_DEV), orow.reshape(1, 16),
                                  ac, ic.reshape(1, D_FF), oc.reshape(1, D_MODEL)), arrays[12:])
        out = final_update(sums, (aw, iw, ow))
        return tuple(o.reshape(-1) if n in (4, 5, 7, 8) else o for n, o in enumerate(out))

    return jax.shard_map(update_all, mesh=mesh, in_specs=in_specs, out_specs=out_specs, check_vma=False)
```

time: 165 us -> 115 us (0.70)
  other arithmetic: 26.5 us -> 0 us
  between operations: 17.5 us -> 0.66 us
  local copies, waits for them, and re-layouts: 7.73 us -> 0 us
  Pallas kernels: 112 us -> 114 us
    reduce_sum x9 -> x0, other arithmetic: 14.6 us -> none  [the longest x2 5.62 us: factored_step(): w_rms = jnp.sqrt(jnp.sum(weight * weight, axis=(-2, -1)) / n_elems)]
    sub x6 -> x0, other arithmetic: 5.06 us -> none  [the longest x2 3.4 us: factored_step(): return (weight - step_coeff[..., None, None] * update, row_new, col_new)]
    slice x3 -> x0, local copies, waits for them, and re-layouts: 3.38 us -> none  [the longest x1 1.79 us: update_all(): w_rms = jnp.sqrt(scal[8 + m] / n_elems)]
    slice x2 -> x0, other arithmetic: 2.81 us -> none  [update_all(): r_new = rows[ROW_AT[m]:ROW_AT[m] + n_loc, 0]]
    unnamed x38 -> x0, local copies, waits for them, and re-layouts: 2.41 us -> none
    another operation x3 -> x0, other arithmetic: 2.05 us -> none  [update_all(): out = [jnp.stack([results[m][k] for m in range(4)]) for k in range(3)]]
    pallas_call x1 -> x2, Pallas kernels: 112 us -> 114 us  [the longest x1 109 us: dense_sums(): pl.pallas_call(dense_kernel, out_shape=shapes_of((N_UNITS,) + block, (176...]
    squeeze x2 -> x0, local copies, waits for them, and re-layouts: 1.84 us -> none  [update_all(): gsum[u]]
where the time goes in v2:
time: 115 us
  Pallas kernels  114 us (99%)
    pallas_call x1, Pallas kernels, dense_sums(): pl.pallas_call(dense_kernel, out_shape=shapes_of((N_UNITS,) + block, (176...  109 us
    pallas_call x1, Pallas kernels, final_update(): pl.pallas_call(final_kernel, out_shape=shapes_of((4, N_DEV, D_MODEL), (4,...  5.6 us

profile of v2, /device:TPU:0, one launch (start us, length us, event | category | flops | bytes accessed | tf_op | source)
XLA Modules:
  0.0 114.8 jit_solution(9490939673615969717)
XLA Ops:
  0.7 108.6 %dense_sums.1 = (f32[20,16,512]{2,1,0:T(8,128)}, f32[176,128]{1,0:T(8,128)}, f32[33,8,128]{2,1,0:T(8,128)}, f32[1024,512]{1,0:T(8,128)}, f32[1,1024]{1,0:T(1,128...) custom-call(bf16[4,32,32,1024]{3,2,1,0:T(8,128)(2,1)} %bitcast.11, ...), custom_call_target="tpu_custom_call" | custom-call | tf_op jit(solution)/shard_map/dense_sums/pallas_call | solution.py:348
  109.2 5.6 %final_update.1 = (f32[4,32,1024]{2,1,0:T(8,128)}, f32[4,32]{1,0:T(4,128)}, f32[4,1024]{1,0:T(4,128)}, f32[32,512]{1,0:T(8,128)}, f32[1,32]{1,0:T(1,128)}, /*ind...) custom-call(f32[20,16,512]{2,1,0:T(8,128)} %get-tuple-element.39.gsu, ...), custom_call_target="tpu_custom_call" | custom-call | tf_op jit(solution)/shard_map/final_update/pallas_call | solution.py:439

commit v3 on v2

v3 whole, which is shorter than its diff:
```python
import functools

import jax
import jax.numpy as jnp
from jax import lax
from jax.experimental import pallas as pl
from jax.experimental.pallas import tpu as pltpu
from jax.sharding import PartitionSpec as P

D_MODEL, D_FF, LANES, N_DEV, TILE = 1024, 512, 128, 32, 8
OPT_STEP = 10
LEARN_RATE = 0.1
EPS_SQUARE = 1e-30
EPS_SCALE = 1e-3
BETA_TWO = 1.0 - OPT_STEP ** -0.8
KEEP = 1.0 - BETA_TWO
F32 = jnp.float32
BLK_R, BLK_C = 16, D_FF
N_UNITS = 20
BIT = {"x": 1, "y": 2, "a": 3, "b": 4}

ORDERS = (
    "xayb", "yaxb", "ayxb", "ayxb", "xyab", "axyb", "xyab", "axyb", "xyab", "yxab",
    "yaxb", "yaxb", "xyab", "yxab", "axyb", "yxab", "axyb", "xayb", "yxab", "xyab",
)
STEP_UNITS = "".join((
    "DRFPQDRINGKPINQHRPMCHALGBKCOBQRFGHSAEJTQJBNOMFAICRNHDIBLEPMN",
    "CHRKFDPBGOIKEJQLGDCBOASFMKTIOJLADQMEJTHKLSEAMNCTGFLOJPSETSTS",
))
STEPS = [(ord(u) - ord("A"), STEP_UNITS[:n].count(u)) for n, u in enumerate(STEP_UNITS)]

UNITS = [(m, 16 * r, D_FF * c) for m in range(4) for r in range(2) for c in range(2)]
UNITS += [(5, 0, 0), (5, 0, D_FF), (4, 0, 0), (4, 16, 0)]
N_ROWS = (D_MODEL, D_MODEL, D_MODEL, D_MODEL, D_MODEL, D_FF)
N_COLS = (D_MODEL, D_MODEL, D_MODEL, D_MODEL, D_FF, D_MODEL)
LOC_ROWS = (N_DEV, N_DEV, N_DEV, N_DEV, N_DEV, 16)
ROW_AT = (0, N_DEV, 64, 96, LANES, 160)
LAST = 4
EARLY = 1
WORK_AT, WORK_EVERY = 16, 3
MESH = pl.DeviceIdType.MESH


def sum_of(value, axis):
    return jnp.sum(value, axis=axis, keepdims=True)


over_rows, over_cols = (functools.partial(sum_of, axis=axis) for axis in range(2))


def sum_all(value):
    return over_rows(over_cols(value))


def step_size(upd_sq, w_sq, n_elems):
    w_rms = jnp.sqrt(w_sq / n_elems)
    return LEARN_RATE * jnp.maximum(EPS_SCALE, w_rms) / jnp.maximum(1.0, jnp.sqrt(upd_sq / n_elems))


def expert_work(loads, arrays, results, sums, factor, acc, out_sem, outs):
    g_v, w_v = arrays[0].at[0], arrays[1].at[0]
    r_old, c_old = arrays[2:]
    w_new, r_new, c_new = results
    n_rows, n_cols = g_v.shape
    c_acc, w_acc, u_acc = (acc.at[n, :, pl.ds(0, n_cols)] for n in range(3))
    quarter = n_rows // 4

    def begin():
        for load in loads:
            load.wait()
        for ref in (c_acc, w_acc, u_acc):
            ref[...] = jnp.zeros((TILE, n_cols), F32)

    def squares(b):
        c_sum, w_sum = c_acc[...], w_acc[...]
        for r in range(16):
            at = slice(LANES * b + TILE * r, LANES * b + TILE * r + TILE)
            sq = g_v[at, :] * g_v[at, :] + EPS_SQUARE
            c_sum = c_sum + sq
            w_sum = w_sum + w_v[at, :] * w_v[at, :]
            sums[TILE * r:TILE * r + TILE, :] = jnp.broadcast_to(over_cols(sq), (TILE, LANES))
        c_acc[...], w_acc[...] = c_sum, w_sum
        part = slice(LANES * b, LANES * b + LANES)
        r_new[:, part] = BETA_TWO * r_old[:, part] + KEEP * (jnp.transpose(sums[...])[0:1, :] / n_cols)

    def factors():
        c_new[...] = BETA_TWO * c_old[...] + KEEP * (over_rows(c_acc[...]) / n_rows)
        mean = over_cols(r_new[...]) / n_rows
        row_factor = lax.rsqrt(r_new[...] / mean)
        for b in range(n_rows // LANES):
            part = slice(LANES * b, LANES * b + LANES)
            factor[part, :] = jnp.transpose(jnp.broadcast_to(row_factor[:, part], (LANES, LANES)))

    def update(q):
        col_factor = lax.rsqrt(c_new[...])

        @pl.loop(0, quarter // N_DEV)
        def _(n):
            at = pl.ds(q * quarter + n * N_DEV, N_DEV)
            upd = g_v[at, :] * factor[at, 0:1] * col_factor
            g_v[at, :] = upd
            sq = upd * upd
            u_acc[...] = u_acc[...] + sq[0:TILE] + sq[TILE:16] + sq[16:24] + sq[24:N_DEV]

    def finish(q):
        coeff = step_size(sum_all(u_acc[...]), sum_all(w_acc[...]), n_rows * n_cols)

        @pl.loop(0, quarter // N_DEV)
        def _(n):
            at = pl.ds(q * quarter + n * N_DEV, N_DEV)
            w_v[at, :] = w_v[at, :] - coeff * g_v[at, :]

        part = pl.ds(q * quarter, quarter)
        outs.append(pltpu.make_async_copy(w_v.at[part], w_new.at[part], out_sem(q)))
        outs[-1].start()

    pieces = [begin] + [functools.partial(squares, b) for b in range(n_rows // LANES)] + [factors]
    return pieces + [functools.partial(f, q) for f in (update, finish) for q in range(4)]


def dense_kernel(attn_g, ffin_g, ffout_g, *refs):
    small, expert_in, refs = refs[:9], refs[9:17], refs[17:]
    (gsum, rows_hbm, stat_hbm), expert_hbm, scratch = refs[:3], refs[3:9], list(refs[9:])
    (row_out, stat_out), scratch = scratch[:2], scratch[2:]
    expert_out = [hbm if n % 3 == 0 else scratch.pop(0) for n, hbm in enumerate(expert_hbm)]
    small_vmem, expert_v, scratch = scratch[:9], scratch[9:17], scratch[17:]
    raw, stage, r0, r1, r2, r3, r4, msg, rx, rb, rx_end, rx_row, tile, end, end_row, g_own, rows_msg, rx_rows, *scratch = scratch
    sums, factor, acc, ld_sem, s_sem, r_sem, x_sem, e_sem, o_sem = scratch
    attn_w, ffin_w, ffout_w, attn_r, ffin_r, ffout_r, attn_c, ffin_c, ffout_c = small_vmem
    me = lax.axis_index("dp")
    bits = [(me // 2 ** k) % 2 for k in range(5)]
    partner = [me + (1 - 2 * bits[k]) * 2 ** k for k in range(5)]
    core = bits[0]
    recvs = (r0, r1, r2, r3, r4)

    def source(u):
        m, row, col = UNITS[u]
        if m < 4:
            return attn_g.at[m, :, pl.ds(row, BLK_R), pl.ds(col, BLK_C)]
        ref = ffin_g if m == 4 else ffout_g
        return ref.at[:, pl.ds(row, BLK_R), pl.ds(col, BLK_C)]

    barrier = pltpu.get_barrier_semaphore()
    for t in range(1, N_DEV):
        pl.semaphore_signal(barrier, inc=1, device_id=((me + t) % N_DEV,), device_id_type=MESH)
    loads = [pltpu.make_async_copy(source(u), raw.at[u], ld_sem.at[u]) for u in range(N_UNITS)]
    stage_zero = [u for u, s in STEPS if s == 0]
    for u in stage_zero[:2]:
        loads[u].start()
    small_loads = [pltpu.make_async_copy(a, b, ld_sem.at[N_UNITS]) for a, b in zip(small, small_vmem)]
    def dest(order, i):
        return sum(((i // 2 ** (3 - j)) % 2) * 2 ** BIT[order[j]] for j in range(4))

    def copy(u, s):
        order = ORDERS[u]
        if s == 0:
            src, to = stage.at[u], partner[0]
        else:
            keep = sum(bits[BIT[order[j]]] * 2 ** (3 - j) for j in range(s - 1))
            k = BIT[order[s - 1]]
            src = r0.at[u, pl.ds(keep + (1 - bits[k]) * 2 ** (4 - s), 2 ** (4 - s))]
            to = partner[k]
        return pltpu.make_async_remote_copy(
            src_ref=src, dst_ref=recvs[s].at[u], send_sem=s_sem.at[s], recv_sem=r_sem.at[s, u],
            device_id=(to,), device_id_type=MESH)

    def block_sum(u, s, i, d):
        total = raw[u, d].astype(F32)
        for j in range(s):
            total = total + recvs[j][u, i % 2 ** (4 - j)]
        return total

    rows_in = (attn_r, attn_r, attn_r, attn_r, ffin_r, ffout_r)
    weights = (attn_w, attn_w, attn_w, attn_w, ffin_w, ffout_w)
    lane = lax.broadcasted_iota(jnp.int32, (1, LANES), 1)

    def statistics(m):
        n_loc, n_col = LOC_ROWS[m], N_COLS[m]
        col_s, col_d = ([0.0] * (n_col // D_FF) for _ in range(2))
        new_rows = []
        total = jnp.zeros((1, 1), F32)
        for h in range(n_loc // 16):
            here = [u for u in range(N_UNITS) if UNITS[u][:2] == (m, 16 * h)]
            squares = {u: g_own[u] * g_own[u] for u in here}
            row_sum = sum(over_cols(squares[u] + EPS_SQUARE) for u in here)
            old = rows_in[m][m:m + 1, :] if m < 4 else rows_in[m][...]
            pick = lax.broadcasted_iota(jnp.int32, (16, n_loc), 0) + 16 * h == lax.broadcasted_iota(
                jnp.int32, (16, n_loc), 1)
            old_col = over_cols(jnp.where(pick, jnp.broadcast_to(old, (16, n_loc)), 0.0))
            new = BETA_TWO * old_col + KEEP * (row_sum / n_col)
            row_out[pl.ds(ROW_AT[m] + 16 * h, 16), :] = jnp.broadcast_to(new, (16, LANES))
            total = total + over_rows(new)
            new_rows.append((new, here, squares))
        mean = total / n_loc
        for new, here, squares in new_rows:
            inv = mean / new
            for u in here:
                c = UNITS[u][2] // D_FF
                col_s[c] = col_s[c] + over_rows(squares[u] + EPS_SQUARE)
                col_d[c] = col_d[c] + over_rows(squares[u] * inv)
        return total, col_s, col_d

    z, rest = me // TILE, me % TILE
    z_order = [TILE * (3 - z), TILE * ((z + 2) % 4), TILE * (z + 1 - 2 * (z % 2)), TILE * z]

    def exchange(k, src_of, dst):
        for n, at in enumerate(z_order):
            @pl.loop(n // 3, TILE)
            def _(r, at=at):
                to = at + (rest + r) % TILE
                pltpu.make_async_remote_copy(
                    src_ref=src_of(to), dst_ref=dst.at[me], send_sem=x_sem.at[2 * k], recv_sem=x_sem.at[2 * k + 1],
                    device_id=(to,), device_id_type=MESH).start()

    def wait_all(sem, dst):
        some = dst.at[pl.ds(0, 31)]
        pltpu.make_async_copy(some, some, x_sem.at[sem]).wait()

    def collect_weights():
        rows_msg[...] = sum(jnp.where(lane == TILE + m, sum_all(w * w), 0.0)
                            for m, w in enumerate(weights[m][m] if m < 4 else weights[m][...] for m in range(6)))
        msg[...] = jnp.zeros((N_DEV, 4, LANES), F32)

    def collect(m):
        total, col_s, col_d = statistics(m)
        for g in range(TILE):
            at = TILE * (m % 5) + g
            row = 0 if m < 4 else 2
            part = slice(LANES * (g % 4), LANES * (g % 4) + LANES)
            msg[at, row:row + 1, :] = col_s[g // 4][:, part]
            msg[at, row + 1:row + 2, :] = col_d[g // 4][:, part]
        rows_msg[...] = rows_msg[...] + jnp.where(lane == m, total, 0.0)

    def send_first():
        exchange(0, lambda to: msg.at[to], rx)
        exchange(4, lambda to: rows_msg, rx_rows)
        rx[me] = msg[me]
        rx_rows[me] = rows_msg[...]

    def lanes_at(k):
        return pl.ds(pl.multiple_of(k * LANES, LANES), LANES)

    def own_groups():
        wait_all(1, rx)
        wait_all(9, rx_rows)
        scal = rx_rows[:, 0, :]
        lanes = lax.broadcasted_iota(jnp.int32, (N_DEV, LANES), 1)

        def group(row, mat, n_row, old):
            sums = over_cols(jnp.where(lanes == mat, scal, 0.0))
            ratio = over_rows(sums) / 32.0 / sums
            new = BETA_TWO * old + KEEP * (over_rows(rx[:, row, :]) / n_row)
            part = over_cols(over_rows(rx[:, row + 1, :] * ratio) / new)
            tile[row // 2:row // 2 + 1, :] = new
            tile[row // 2 + 2:row // 2 + 3, :] = jnp.broadcast_to(part, (1, LANES))

        here = lanes_at(me % TILE)
        group(0, me // TILE, 1024.0, sum(jnp.where(me // TILE == m, attn_c[m:m + 1, here], 0.0) for m in range(4)))
        group(2, 5, 512.0, ffout_c[:, here])
        exchange(1, lambda to: tile, rb)
        rb[me] = tile[...]
        stat_out[N_DEV, 0:1, :] = over_rows(scal)

    def send_last():
        total, (col_s,), (col_d,) = statistics(LAST)
        for g in range(4):
            part = slice(LANES * g, LANES * g + LANES)
            end[g:g + 1, :] = col_s[:, part]
            end[g + 4:g + 5, :] = col_d[:, part]
        end_row[...] = jnp.broadcast_to(total, (1, LANES))
        exchange(2, lambda to: end, rx_end)
        exchange(3, lambda to: end_row, rx_row)
        rx_end[me] = end[...]
        rx_row[me] = end_row[...]

    def take_last():
        wait_all(5, rx_end)
        wait_all(7, rx_row)
        rows_all = rx_row[:, 0, :]
        grand = over_rows(rows_all)
        ratio = grand / 32.0 / rows_all
        is_s = lax.broadcasted_iota(jnp.int32, (TILE, LANES), 0) < 4
        both = [jnp.zeros((TILE, LANES), F32) for _ in range(4)]
        for p in range(N_DEV):
            both[p % 4] = both[p % 4] + rx_end[p] * jnp.where(is_s, 1.0, ratio[p:p + 1, :])
        both = (both[0] + both[1]) + (both[2] + both[3])
        col_s, col_d = both[0:4, :], both[4:TILE, :]
        for g in range(4):
            stat_out[33, g:g + 1, :] = ffin_c[:, LANES * g:LANES * g + LANES]
        new = BETA_TWO * stat_out[33, 0:4, :] + KEEP * (col_s / 1024.0)
        stat_out[33, 0:4, :] = new
        stat_out[33, 4:5, :] = jnp.broadcast_to(sum_all(col_d / new), (1, LANES))
        stat_out[33, 5:6, :] = grand

    outs = []

    def put(src, dst, n):
        outs.append(pltpu.make_async_copy(src, dst, o_sem.at[n]))
        outs[-1].start()

    def to_f32(u):
        loads[u].wait()

        @pl.loop(0, 4)
        def _(n):
            for k in range(4):
                i = 4 * n + k
                stage[u, i] = raw[u, dest(ORDERS[u], i) + 1 - core].astype(F32)

    def step(u, s):
        order = ORDERS[u]
        if s == 0:
            to_f32(u)
        else:
            copy(u, s - 1).wait_recv()
            base = sum(bits[BIT[order[j]]] * 2 ** (3 - j) for j in range(min(s - 1, 4)))
            if s == 5:
                g_own[u] = block_sum(u, 5, base, me) * (1.0 / 32.0)
                outs.append(pltpu.make_async_copy(g_own.at[u], gsum.at[u], ld_sem.at[u]))
                outs[-1].start()
                return
            base = base + (1 - bits[BIT[order[s - 1]]]) * 2 ** (4 - s)

            @pl.loop(0, 2 ** (4 - s))
            def _(n):
                i = base + n
                r0[u, i] = block_sum(u, s, i, dest(order, i) + core)
        copy(u, s).start()

    for u in stage_zero[2:TILE]:
        loads[u].start()
    for u in stage_zero[:EARLY]:
        to_f32(u)
    pl.semaphore_wait(barrier, 31)
    for u in stage_zero[:EARLY]:
        copy(u, 0).start()
    for u in stage_zero[TILE:]:
        loads[u].start()
    expert_loads = [pltpu.make_async_copy(a, b, e_sem.at[n]) for n, (a, b) in enumerate(zip(expert_in, expert_v))]
    work = []
    for k in range(2):
        half = slice(4 * k, 4 * k + 4)
        work += expert_work(expert_loads[half], expert_v[half], expert_out[3 * k:3 * k + 3], sums, factor,
                            acc.at[k], lambda n, k=k: e_sem.at[TILE + 4 * k + n], outs)
    left = {m: sum(unit[0] == m for unit in UNITS) for m in range(6)}
    for n, (u, s) in enumerate(STEPS):
        if n == WORK_AT - 4:
            for load in small_loads + expert_loads:
                load.start()
            for load in small_loads:
                load.wait()
            collect_weights()
        if s > 0 or u not in stage_zero[:EARLY]:
            step(u, s)
        if n >= WORK_AT and n % WORK_EVERY == 0 and work:
            work.pop(0)()
        if n == len(STEPS) - TILE:
            for piece in work:
                piece()
        if s == 5:
            m = UNITS[u][0]
            left[m] -= 1
            if left[m] == 0 and m != LAST:
                collect(m)
            if s == 5 and sum(left.values()) == left[LAST] and m != LAST:
                send_first()
    send_last()
    put(row_out, rows_hbm, 0)
    for n in range(6):
        if n % 3:
            put(expert_out[n], expert_hbm[n], n)
    own_groups()

    for k, sent in enumerate((stage, r1, r2, r3, r4)):
        pltpu.make_async_copy(sent, sent, s_sem.at[k]).wait()
    for out in outs:
        out.wait()
    take_last()
    wait_all(3, rb)
    stat_out[pl.ds(0, N_DEV), 0:4, :] = rb[...]
    put(stat_out, stat_hbm, 3)
    outs[-1].wait()
    for k, ref in ((0, msg), (2, rb), (4, rx_end), (6, rx_row), (TILE, rx_rows)):
        wait_all(k, ref)


ANY = pl.BlockSpec(memory_space=pl.ANY)
VMEM = pl.BlockSpec(memory_space=pltpu.VMEM)


EXPERT_SHAPES = ((D_MODEL, D_FF), (1, D_MODEL), (1, D_FF), (D_FF, D_MODEL), (1, D_FF), (1, D_MODEL))


def shapes_of(*shapes):
    return tuple(jax.ShapeDtypeStruct(shape, F32) for shape in shapes)


def dense_sums(grads, small, experts):
    block = (BLK_R, BLK_C)
    vectors = tuple(shape for n, shape in enumerate(EXPERT_SHAPES) if n % 3)
    halves = [pltpu.VMEM((N_UNITS, 2 ** k) + block, F32) for k in (4, 4, 3, 2, 1, 0)]
    return pl.pallas_call(
        dense_kernel,
        out_shape=shapes_of((N_UNITS,) + block, (176, LANES), (34, TILE, LANES), *EXPERT_SHAPES),
        in_specs=[ANY] * 20,
        out_specs=(ANY,) * 9,
        scratch_shapes=[pltpu.VMEM(shape, F32) for shape in ((176, LANES), (34, TILE, LANES)) + vectors] + [
            pltpu.VMEM(a.shape, F32) for a in small + experts] + [
            pltpu.VMEM((N_UNITS, N_DEV) + block, jnp.bfloat16), *halves,
            *[pltpu.VMEM((N_DEV, 4, LANES), F32)] * 3, pltpu.VMEM((N_DEV, TILE, LANES), F32), pltpu.VMEM((N_DEV, 1, LANES), F32),
            pltpu.VMEM((4, LANES), F32), pltpu.VMEM((TILE, LANES), F32), pltpu.VMEM((1, LANES), F32),
            pltpu.VMEM((N_UNITS,) + block, F32), pltpu.VMEM((1, LANES), F32), pltpu.VMEM((N_DEV, 1, LANES), F32),
            pltpu.VMEM((LANES, LANES), F32), pltpu.VMEM((D_MODEL, LANES), F32), pltpu.VMEM((2, 3, TILE, D_MODEL), F32),
            pltpu.SemaphoreType.DMA((N_UNITS + 1,)),
            pltpu.SemaphoreType.DMA((5,)), pltpu.SemaphoreType.DMA((5, N_UNITS)),
            pltpu.SemaphoreType.DMA((10,)),
            pltpu.SemaphoreType.DMA((16,)),
            pltpu.SemaphoreType.DMA((7,)),
        ],
        compiler_params=pltpu.CompilerParams(
            has_side_effects=True, vmem_limit_bytes=58 * 2 ** 20, collective_id=1),
        name="dense_sums",
    )(*grads, *small, *experts)


def final_kernel(gsum, rows_in, stat_in, *refs):
    dense_w, expert_in, refs = refs[:3], refs[3:9], refs[9:]
    (aw_new, ar_new, ac_new, iw_new, ir_new, ic_new, ow_new, or_new, oc_new), refs = refs[:9], refs[9:]
    expert_out, (gs_v, rows, stat, aw, iw, ow, *expert_v), (in_sem, out_sem) = refs[:6], refs[6:-2], refs[-2:]

    dense_loads = [pltpu.make_async_copy(a, b, in_sem.at[n]) for n, (a, b) in enumerate(
        zip((stat_in, rows_in, gsum) + dense_w, (stat, rows, gs_v, aw, iw, ow)))]
    moves = []
    for k in range(6):
        src, via, dst = expert_in[k], expert_v[k], expert_out[k]
        n_parts = 1 if k % 3 else 4
        n_rows = via.shape[0] // n_parts
        for q in range(n_parts):
            part = pl.ds(q * n_rows, n_rows)
            at = len(moves)
            moves.append((pltpu.make_async_copy(src.at[part], via.at[part], in_sem.at[6 + at]),
                          pltpu.make_async_copy(via.at[part], dst.at[part] if n_parts == 1 else dst.at[0, part],
                                                out_sem.at[3 + at])))
    for load in dense_loads:
        load.start()
    for load, _ in moves:
        load.start()
    for load in dense_loads:
        load.wait()

    scal = stat[N_DEV, 0:1, :]
    lane = lax.broadcasted_iota(jnp.int32, (1, LANES), 1)
    flipped = (jnp.transpose(rows[0:LANES, :]), jnp.transpose(rows[48:176, :]))
    for m in range(4):
        ar_new[m:m + 1, :] = flipped[0][0:1, N_DEV * m:N_DEV * m + N_DEV]
    ir_new[...] = flipped[1][0:1, 80:112]
    or_new[...] = flipped[1][0:1, 112:LANES]
    outs = []
    for m in range(6):
        row = m // 5
        row_total = over_cols(jnp.where(lane == m, scal, 0.0))
        if m == LAST:
            c_new = jnp.concatenate([stat[33, g:g + 1, :] for g in range(4)], axis=1)
            parts, row_total = stat[33, 4:5, 0:1], stat[33, 5:6, 0:1]
        else:
            c_new = jnp.concatenate([stat[TILE * (m % 5) + g, row:row + 1, :] for g in range(TILE)], axis=1)
            parts = sum(stat[TILE * (m % 5) + g, row + 2:row + 3, 0:1] for g in range(TILE))
        if m < 4:
            ac_new[m:m + 1, :] = c_new
        else:
            (ic_new, oc_new)[m - 4][...] = c_new
        w_sq = over_cols(jnp.where(lane == TILE + m, scal, 0.0))
        coeff = step_size(parts, w_sq, N_ROWS[m] * N_COLS[m])
        col_factor = lax.rsqrt(c_new)
        w = aw.at[m] if m < 4 else (iw, ow)[m - 4]
        for u in range(N_UNITS):
            if UNITS[u][0] != m:
                continue
            r_at, c_at = UNITS[u][1:]
            r_factor = lax.rsqrt(rows[ROW_AT[m] + r_at:ROW_AT[m] + r_at + BLK_R, 0:1] / (row_total / N_ROWS[m]))
            step = coeff * (gs_v[u] * r_factor * col_factor[:, c_at:c_at + BLK_C])
            part = (slice(r_at, r_at + BLK_R), slice(c_at, c_at + BLK_C))
            w[part] = w[part] - step
        if m >= 3:
            outs.append(pltpu.make_async_copy((aw, iw, ow)[m - 3], (aw_new, iw_new, ow_new)[m - 3],
                                              out_sem.at[m - 3]))
            outs[-1].start()
    for load, out in moves:
        load.wait()
        out.start()
        outs.append(out)
    for out in outs:
        out.wait()


def final_update(sums, dense_w):
    experts = [(1,) + shape if shape[0] > 1 else shape for shape in EXPERT_SHAPES]
    return pl.pallas_call(
        final_kernel,
        out_shape=shapes_of((4, N_DEV, D_MODEL), (4, N_DEV), (4, D_MODEL), (N_DEV, D_FF), (1, N_DEV), (1, D_FF), (16, D_MODEL), (1, 16),
                            (1, D_MODEL), *experts),
        in_specs=[ANY] * 12,
        out_specs=[ANY, VMEM, VMEM] * 3 + [ANY] * 6,
        scratch_shapes=[
            *[pltpu.VMEM(a.shape, F32) for a in (*sums[:3], *dense_w, *sums[3:])],
            pltpu.SemaphoreType.DMA((18,)), pltpu.SemaphoreType.DMA((15,)),
        ],
        compiler_params=pltpu.CompilerParams(vmem_limit_bytes=67043328),
        name="final_update",
    )(*sums[:3], *dense_w, *sums[3:])


def solution(mesh):
    dense_specs = (
        (P("dp"), P(None, "dp", None), P(None, "dp"), P()),
        (P("dp"), P("dp", None), P("dp"), P()),
        (P("dp"), P("dp", None), P("dp"), P()),
    )
    expert_specs = ((P("dp"), P("dp"), P("dp"), P("dp")),) * 2
    all_specs = dense_specs + expert_specs
    in_specs = tuple(part_spec for group in all_specs for part_spec in group)
    out_specs = tuple(part_spec for group in all_specs for part_spec in group[1:])

    def update_all(*arrays):
        (ag, aw, ar, ac, ig, iw, ir, ic, og, ow, orow, oc) = arrays[:12]
        grads = (ag.reshape(4, N_DEV, N_DEV, D_MODEL), ig.reshape(N_DEV, N_DEV, D_FF), og.reshape(N_DEV, 16, D_MODEL))
        sums = dense_sums(grads, (aw, iw, ow, ar, ir.reshape(1, N_DEV), orow.reshape(1, 16),
                                  ac, ic.reshape(1, D_FF), oc.reshape(1, D_MODEL)), arrays[12:])
        out = final_update(sums, (aw, iw, ow))
        return tuple(o.reshape(-1) if n in (4, 5, 7, TILE) else o for n, o in enumerate(out))

    return jax.shard_map(update_all, mesh=mesh, in_specs=in_specs, out_specs=out_specs, check_vma=False)
```

time: 115 us -> 106 us (0.922)
  Pallas kernels: 114 us -> 106 us
    pallas_call x1, Pallas kernels: 109 us -> 101 us  [dense_sums(): pl.pallas_call(dense_kernel, out_shape=shapes_of((N_UNITS,) + block, (176...]
where the time goes in v3:
time: 106 us
  Pallas kernels  106 us (100%)
    pallas_call x1, Pallas kernels, dense_sums(): pl.pallas_call(dense_kernel, out_shape=shapes_of((N_UNITS,) + block, (176...  101 us
    pallas_call x1, Pallas kernels, final_update(): pl.pallas_call(final_kernel, out_shape=shapes_of((4, N_DEV, D_MODEL), (4,...  4.84 us

profile of v3, /device:TPU:0, one launch (start us, length us, event | category | flops | bytes accessed | tf_op | source)
XLA Modules:
  0.0 106.2 jit_solution(610027243135976979)
XLA Ops:
  0.7 100.7 %dense_sums.1 = (f32[20,16,512]{2,1,0:T(8,128)}, f32[176,128]{1,0:T(8,128)}, f32[34,8,128]{2,1,0:T(8,128)}, f32[1024,512]{1,0:T(8,128)}, f32[1,1024]{1,0:T(1,128...) custom-call(bf16[4,32,32,1024]{3,2,1,0:T(8,128)(2,1)} %bitcast.11, ...), custom_call_target="tpu_custom_call" | custom-call | tf_op jit(solution)/shard_map/dense_sums/pallas_call | solution.py:402
  101.4 4.8 %final_update.1 = (f32[4,32,1024]{2,1,0:T(8,128)}, f32[4,32]{1,0:T(4,128)}, f32[4,1024]{1,0:T(4,128)}, f32[32,512]{1,0:T(8,128)}, f32[1,32]{1,0:T(1,128)}, /*ind...) custom-call(f32[20,16,512]{2,1,0:T(8,128)} %get-tuple-element.39.gsu, ...), custom_call_target="tpu_custom_call" | custom-call | tf_op jit(solution)/shard_map/final_update/pallas_call | solution.py:498

commit v4 on v3

--- a/solution.py
+++ b/solution.py
@@ -57,10 +57,9 @@
     return LEARN_RATE * jnp.maximum(EPS_SCALE, w_rms) / jnp.maximum(1.0, jnp.sqrt(upd_sq / n_elems))
 
 
-def expert_work(loads, arrays, results, sums, factor, acc, out_sem, outs):
-    g_v, w_v = arrays[0].at[0], arrays[1].at[0]
-    r_old, c_old = arrays[2:]
-    w_new, r_new, c_new = results
+def expert_work(loads, arrays, results, sums, factor, acc):
+    g_v, w_v, r_old, c_old = arrays
+    r_new, c_new = results
     n_rows, n_cols = g_v.shape
     c_acc, w_acc, u_acc = (acc.at[n, :, pl.ds(0, n_cols)] for n in range(3))
     quarter = n_rows // 4
@@ -110,22 +109,18 @@
             at = pl.ds(q * quarter + n * N_DEV, N_DEV)
             w_v[at, :] = w_v[at, :] - coeff * g_v[at, :]
 
-        part = pl.ds(q * quarter, quarter)
-        outs.append(pltpu.make_async_copy(w_v.at[part], w_new.at[part], out_sem(q)))
-        outs[-1].start()
-
     pieces = [begin] + [functools.partial(squares, b) for b in range(n_rows // LANES)] + [factors]
     return pieces + [functools.partial(f, q) for f in (update, finish) for q in range(4)]
 
 
 def dense_kernel(attn_g, ffin_g, ffout_g, *refs):
     small, expert_in, refs = refs[:9], refs[9:17], refs[17:]
-    (gsum, rows_hbm, stat_hbm), expert_hbm, scratch = refs[:3], refs[3:9], list(refs[9:])
-    (row_out, stat_out), scratch = scratch[:2], scratch[2:]
-    expert_out = [hbm if n % 3 == 0 else scratch.pop(0) for n, hbm in enumerate(expert_hbm)]
-    small_vmem, expert_v, scratch = scratch[:9], scratch[9:17], scratch[17:]
-    raw, stage, r0, r1, r2, r3, r4, msg, rx, rb, rx_end, rx_row, tile, end, end_row, g_own, rows_msg, rx_rows, *scratch = scratch
-    sums, factor, acc, ld_sem, s_sem, r_sem, x_sem, e_sem, o_sem = scratch
+    (g_own, row_out, stat_out), dense_w, expert_out, scratch = refs[:3], refs[3:6], refs[6:12], refs[12:]
+    small_vmem, (g_in, *states_in), (g_out, *states_out), scratch = (
+        dense_w + scratch[:6], scratch[6:9], scratch[9:12], scratch[12:])
+    expert_v = (g_in, expert_out[0], *states_in, g_out, expert_out[3], *states_out)
+    raw, stage, r0, r1, r2, r3, r4, msg, rx, rb, rx_end, rx_row, tile, end, end_row, rows_msg, rx_rows, *scratch = scratch
+    sums, factor, acc, ld_sem, s_sem, r_sem, x_sem, e_sem = scratch
     attn_w, ffin_w, ffout_w, attn_r, ffin_r, ffout_r, attn_c, ffin_c, ffout_c = small_vmem
     me = lax.axis_index("dp")
     bits = [(me // 2 ** k) % 2 for k in range(5)]
@@ -292,12 +287,6 @@
         stat_out[33, 4:5, :] = jnp.broadcast_to(sum_all(col_d / new), (1, LANES))
         stat_out[33, 5:6, :] = grand
 
-    outs = []
-
-    def put(src, dst, n):
-        outs.append(pltpu.make_async_copy(src, dst, o_sem.at[n]))
-        outs[-1].start()
-
     def to_f32(u):
         loads[u].wait()
 
@@ -316,8 +305,6 @@
             base = sum(bits[BIT[order[j]]] * 2 ** (3 - j) for j in range(min(s - 1, 4)))
             if s == 5:
                 g_own[u] = block_sum(u, 5, base, me) * (1.0 / 32.0)
-                outs.append(pltpu.make_async_copy(g_own.at[u], gsum.at[u], ld_sem.at[u]))
-                outs[-1].start()
                 return
             base = base + (1 - bits[BIT[order[s - 1]]]) * 2 ** (4 - s)
 
@@ -336,12 +323,12 @@
         copy(u, 0).start()
     for u in stage_zero[TILE:]:
         loads[u].start()
-    expert_loads = [pltpu.make_async_copy(a, b, e_sem.at[n]) for n, (a, b) in enumerate(zip(expert_in, expert_v))]
+    expert_loads = [pltpu.make_async_copy(a.at[0] if n % 4 < 2 else a, b, e_sem.at[n])
+                    for n, (a, b) in enumerate(zip(expert_in, expert_v))]
     work = []
     for k in range(2):
         half = slice(4 * k, 4 * k + 4)
-        work += expert_work(expert_loads[half], expert_v[half], expert_out[3 * k:3 * k + 3], sums, factor,
-                            acc.at[k], lambda n, k=k: e_sem.at[TILE + 4 * k + n], outs)
+        work += expert_work(expert_loads[half], expert_v[half], expert_out[3 * k + 1:3 * k + 3], sums, factor, acc.at[k])
     left = {m: sum(unit[0] == m for unit in UNITS) for m in range(6)}
     for n, (u, s) in enumerate(STEPS):
         if n == WORK_AT - 4:
@@ -365,21 +352,13 @@
             if s == 5 and sum(left.values()) == left[LAST] and m != LAST:
                 send_first()
     send_last()
-    put(row_out, rows_hbm, 0)
-    for n in range(6):
-        if n % 3:
-            put(expert_out[n], expert_hbm[n], n)
     own_groups()
 
     for k, sent in enumerate((stage, r1, r2, r3, r4)):
         pltpu.make_async_copy(sent, sent, s_sem.at[k]).wait()
-    for out in outs:
-        out.wait()
     take_last()
     wait_all(3, rb)
     stat_out[pl.ds(0, N_DEV), 0:4, :] = rb[...]
-    put(stat_out, stat_hbm, 3)
-    outs[-1].wait()
     for k, ref in ((0, msg), (2, rb), (4, rx_end), (6, rx_row), (TILE, rx_rows)):
         wait_all(k, ref)
 
@@ -395,58 +374,45 @@
     return tuple(jax.ShapeDtypeStruct(shape, F32) for shape in shapes)
 
 
+def in_vmem(*shapes):
+    return tuple(pltpu.VMEM(shape, F32) for shape in shapes)
+
+
 def dense_sums(grads, small, experts):
     block = (BLK_R, BLK_C)
-    vectors = tuple(shape for n, shape in enumerate(EXPERT_SHAPES) if n % 3)
     halves = [pltpu.VMEM((N_UNITS, 2 ** k) + block, F32) for k in (4, 4, 3, 2, 1, 0)]
     return pl.pallas_call(
         dense_kernel,
-        out_shape=shapes_of((N_UNITS,) + block, (176, LANES), (34, TILE, LANES), *EXPERT_SHAPES),
+        out_shape=in_vmem((N_UNITS,) + block, (176, LANES), (34, TILE, LANES), *[a.shape for a in small[:3]], *EXPERT_SHAPES),
         in_specs=[ANY] * 20,
-        out_specs=(ANY,) * 9,
-        scratch_shapes=[pltpu.VMEM(shape, F32) for shape in ((176, LANES), (34, TILE, LANES)) + vectors] + [
-            pltpu.VMEM(a.shape, F32) for a in small + experts] + [
+        out_specs=(VMEM,) * 12,
+        scratch_shapes=[pltpu.VMEM(a.shape, F32) for a in small[3:]] + [
+            pltpu.VMEM(a.shape[-2:], F32) for n, a in enumerate(experts) if n % 4 != 1] + [
             pltpu.VMEM((N_UNITS, N_DEV) + block, jnp.bfloat16), *halves,
             *[pltpu.VMEM((N_DEV, 4, LANES), F32)] * 3, pltpu.VMEM((N_DEV, TILE, LANES), F32), pltpu.VMEM((N_DEV, 1, LANES), F32),
             pltpu.VMEM((4, LANES), F32), pltpu.VMEM((TILE, LANES), F32), pltpu.VMEM((1, LANES), F32),
-            pltpu.VMEM((N_UNITS,) + block, F32), pltpu.VMEM((1, LANES), F32), pltpu.VMEM((N_DEV, 1, LANES), F32),
+            pltpu.VMEM((1, LANES), F32), pltpu.VMEM((N_DEV, 1, LANES), F32),
             pltpu.VMEM((LANES, LANES), F32), pltpu.VMEM((D_MODEL, LANES), F32), pltpu.VMEM((2, 3, TILE, D_MODEL), F32),
             pltpu.SemaphoreType.DMA((N_UNITS + 1,)),
             pltpu.SemaphoreType.DMA((5,)), pltpu.SemaphoreType.DMA((5, N_UNITS)),
             pltpu.SemaphoreType.DMA((10,)),
-            pltpu.SemaphoreType.DMA((16,)),
-            pltpu.SemaphoreType.DMA((7,)),
+            pltpu.SemaphoreType.DMA((TILE,)),
         ],
         compiler_params=pltpu.CompilerParams(
-            has_side_effects=True, vmem_limit_bytes=58 * 2 ** 20, collective_id=1),
+            has_side_effects=True, vmem_limit_bytes=52 * 2 ** 20, collective_id=1),
         name="dense_sums",
     )(*grads, *small, *experts)
 
 
-def final_kernel(gsum, rows_in, stat_in, *refs):
-    dense_w, expert_in, refs = refs[:3], refs[3:9], refs[9:]
+def final_kernel(gs_v, rows, stat, *refs):
+    (aw, iw, ow), expert_in, refs = refs[:3], refs[3:9], refs[9:]
     (aw_new, ar_new, ac_new, iw_new, ir_new, ic_new, ow_new, or_new, oc_new), refs = refs[:9], refs[9:]
-    expert_out, (gs_v, rows, stat, aw, iw, ow, *expert_v), (in_sem, out_sem) = refs[:6], refs[6:-2], refs[-2:]
-
-    dense_loads = [pltpu.make_async_copy(a, b, in_sem.at[n]) for n, (a, b) in enumerate(
-        zip((stat_in, rows_in, gsum) + dense_w, (stat, rows, gs_v, aw, iw, ow)))]
-    moves = []
-    for k in range(6):
-        src, via, dst = expert_in[k], expert_v[k], expert_out[k]
-        n_parts = 1 if k % 3 else 4
-        n_rows = via.shape[0] // n_parts
-        for q in range(n_parts):
-            part = pl.ds(q * n_rows, n_rows)
-            at = len(moves)
-            moves.append((pltpu.make_async_copy(src.at[part], via.at[part], in_sem.at[6 + at]),
-                          pltpu.make_async_copy(via.at[part], dst.at[part] if n_parts == 1 else dst.at[0, part],
-                                                out_sem.at[3 + at])))
-    for load in dense_loads:
-        load.start()
-    for load, _ in moves:
-        load.start()
-    for load in dense_loads:
-        load.wait()
+    expert_out, updated, out_sem = refs[:6], refs[6:9], refs[9]
+
+    outs = [pltpu.make_async_copy(a, b if k % 3 else b.at[0], out_sem.at[3 + k])
+            for k, (a, b) in enumerate(zip(expert_in, expert_out))]
+    for out in outs:
+        out.start()
 
     scal = stat[N_DEV, 0:1, :]
     lane = lax.broadcasted_iota(jnp.int32, (1, LANES), 1)
@@ -455,7 +421,6 @@
         ar_new[m:m + 1, :] = flipped[0][0:1, N_DEV * m:N_DEV * m + N_DEV]
     ir_new[...] = flipped[1][0:1, 80:112]
     or_new[...] = flipped[1][0:1, 112:LANES]
-    outs = []
     for m in range(6):
         row = m // 5
         row_total = over_cols(jnp.where(lane == m, scal, 0.0))
@@ -480,34 +445,27 @@
             r_factor = lax.rsqrt(rows[ROW_AT[m] + r_at:ROW_AT[m] + r_at + BLK_R, 0:1] / (row_total / N_ROWS[m]))
             step = coeff * (gs_v[u] * r_factor * col_factor[:, c_at:c_at + BLK_C])
             part = (slice(r_at, r_at + BLK_R), slice(c_at, c_at + BLK_C))
-            w[part] = w[part] - step
+            new = updated[0].at[m] if m < 4 else updated[m - 3]
+            new[part] = w[part] - step
         if m >= 3:
-            outs.append(pltpu.make_async_copy((aw, iw, ow)[m - 3], (aw_new, iw_new, ow_new)[m - 3],
-                                              out_sem.at[m - 3]))
+            outs.append(pltpu.make_async_copy(updated[m - 3], (aw_new, iw_new, ow_new)[m - 3], out_sem.at[m - 3]))
             outs[-1].start()
-    for load, out in moves:
-        load.wait()
-        out.start()
-        outs.append(out)
     for out in outs:
         out.wait()
 
 
-def final_update(sums, dense_w):
+def final_update(sums):
     experts = [(1,) + shape if shape[0] > 1 else shape for shape in EXPERT_SHAPES]
     return pl.pallas_call(
         final_kernel,
         out_shape=shapes_of((4, N_DEV, D_MODEL), (4, N_DEV), (4, D_MODEL), (N_DEV, D_FF), (1, N_DEV), (1, D_FF), (16, D_MODEL), (1, 16),
                             (1, D_MODEL), *experts),
-        in_specs=[ANY] * 12,
+        in_specs=[VMEM] * 12,
         out_specs=[ANY, VMEM, VMEM] * 3 + [ANY] * 6,
-        scratch_shapes=[
-            *[pltpu.VMEM(a.shape, F32) for a in (*sums[:3], *dense_w, *sums[3:])],
-            pltpu.SemaphoreType.DMA((18,)), pltpu.SemaphoreType.DMA((15,)),
-        ],
-        compiler_params=pltpu.CompilerParams(vmem_limit_bytes=67043328),
+        scratch_shapes=[*in_vmem(*[a.shape for a in sums[3:6]]), pltpu.SemaphoreType.DMA((9,))],
+        compiler_params=pltpu.CompilerParams(vmem_limit_bytes=TILE * 2 ** 20),
         name="final_update",
-    )(*sums[:3], *dense_w, *sums[3:])
+    )(*sums)
 
 
 def solution(mesh):
@@ -526,7 +484,7 @@
         grads = (ag.reshape(4, N_DEV, N_DEV, D_MODEL), ig.reshape(N_DEV, N_DEV, D_FF), og.reshape(N_DEV, 16, D_MODEL))
         sums = dense_sums(grads, (aw, iw, ow, ar, ir.reshape(1, N_DEV), orow.reshape(1, 16),
                                   ac, ic.reshape(1, D_FF), oc.reshape(1, D_MODEL)), arrays[12:])
-        out = final_update(sums, (aw, iw, ow))
+        out = final_update(sums)
         return tuple(o.reshape(-1) if n in (4, 5, 7, TILE) else o for n, o in enumerate(out))
 
     return jax.shard_map(update_all, mesh=mesh, in_specs=in_specs, out_specs=out_specs, check_vma=False)

time: 106 us -> 104 us (0.981)
  Pallas kernels: 106 us -> 103 us
    pallas_call x1, Pallas kernels: 4.84 us -> 3.13 us  [final_update(): pl.pallas_call(final_kernel, out_shape=shapes_of((4, N_DEV, D_MODEL), (4,...]
where the time goes in v4:
time: 104 us
  Pallas kernels  103 us (99%)
    pallas_call x1, Pallas kernels, dense_sums(): pl.pallas_call(dense_kernel, out_shape=in_vmem((N_UNITS,) + block, (176,...  100 us
    pallas_call x1, Pallas kernels, final_update(): pl.pallas_call(final_kernel, out_shape=shapes_of((4, N_DEV, D_MODEL), (4,...  3.13 us

profile of v4, /device:TPU:0, one launch (start us, length us, event | category | flops | bytes accessed | tf_op | source)
XLA Modules:
  0.0 103.8 jit_solution(13291189068690518962)
XLA Ops:
  0.7 100.0 %dense_sums.1 = (f32[20,16,512]{2,1,0:T(8,128)S(1)}, f32[176,128]{1,0:T(8,128)S(1)}, f32[34,8,128]{2,1,0:T(8,128)S(1)}, f32[4,32,1024]{2,1,0:T(8,128)S(1)}, f32[...) custom-call(bf16[4,32,32,1024]{3,2,1,0:T(8,128)(2,1)} %bitcast.11, ...), custom_call_target="tpu_custom_call" | custom-call | tf_op jit(solution)/shard_map/dense_sums/pallas_call | solution.py:384
  100.6 3.1 %final_update.1 = (f32[4,32,1024]{2,1,0:T(8,128)}, f32[4,32]{1,0:T(4,128)}, f32[4,1024]{1,0:T(4,128)}, f32[32,512]{1,0:T(8,128)}, f32[1,32]{1,0:T(1,128)}, /*ind...) custom-call(f32[20,16,512]{2,1,0:T(8,128)S(1)} %get-tuple-element.42, ...), custom_call_target="tpu_custom_call" | custom-call | tf_op jit(solution)/shard_map/final_update/pallas_call | solution.py:459

commit v5 on v4

--- a/solution.py
+++ b/solution.py
@@ -20,12 +20,12 @@
 BIT = {"x": 1, "y": 2, "a": 3, "b": 4}
 
 ORDERS = (
-    "xayb", "yaxb", "ayxb", "ayxb", "xyab", "axyb", "xyab", "axyb", "xyab", "yxab",
-    "yaxb", "yaxb", "xyab", "yxab", "axyb", "yxab", "axyb", "xayb", "yxab", "xyab",
+    "xyab", "yaxb", "xyab", "xayb", "xyab", "yxab", "ayxb", "axyb", "yaxb", "yaxb",
+    "ayxb", "yaxb", "xyab", "xayb", "ayxb", "xayb", "ayxb", "xyab", "xyab", "yxab",
 )
 STEP_UNITS = "".join((
-    "DRFPQDRINGKPINQHRPMCHALGBKCOBQRFGHSAEJTQJBNOMFAICRNHDIBLEPMN",
-    "CHRKFDPBGOIKEJQLGDCBOASFMKTIOJLADQMEJTHKLSEAMNCTGFLOJPSETSTS",
+    "NHFIMJNBHFQMQJLNKROHAROBACJFITKLGNGECDDHJKPELAFNMGIBDHCLKIAQ",
+    "PBFGMEORLCAJTQSEMLCSKIPEDBRAOQMPGNTDCRSOFIPJGTDHBQKRSEOPTSTS",
 ))
 STEPS = [(ord(u) - ord("A"), STEP_UNITS[:n].count(u)) for n, u in enumerate(STEP_UNITS)]
 
@@ -36,7 +36,7 @@
 LOC_ROWS = (N_DEV, N_DEV, N_DEV, N_DEV, N_DEV, 16)
 ROW_AT = (0, N_DEV, 64, 96, LANES, 160)
 LAST = 4
-EARLY = 1
+EARLY = 2
 WORK_AT, WORK_EVERY = 16, 3
 MESH = pl.DeviceIdType.MESH
 

time: 104 us -> 104 us (level)
  no operation moved by 1% of the time
where the time goes in v5:
time: 104 us
  Pallas kernels  103 us (99%)
    pallas_call x1, Pallas kernels, dense_sums(): pl.pallas_call(dense_kernel, out_shape=in_vmem((N_UNITS,) + block, (176,...  99.8 us
    pallas_call x1, Pallas kernels, final_update(): pl.pallas_call(final_kernel, out_shape=shapes_of((4, N_DEV, D_MODEL), (4,...  3.13 us

profile of v5, /device:TPU:0, one launch (start us, length us, event | category | flops | bytes accessed | tf_op | source)
XLA Modules:
  0.0 103.6 jit_solution(3656919468877871959)
XLA Ops:
  0.7 99.8 %dense_sums.1 = (f32[20,16,512]{2,1,0:T(8,128)S(1)}, f32[176,128]{1,0:T(8,128)S(1)}, f32[34,8,128]{2,1,0:T(8,128)S(1)}, f32[4,32,1024]{2,1,0:T(8,128)S(1)}, f32[...) custom-call(bf16[4,32,32,1024]{3,2,1,0:T(8,128)(2,1)} %bitcast.11, ...), custom_call_target="tpu_custom_call" | custom-call | tf_op jit(solution)/shard_map/dense_sums/pallas_call | solution.py:384
  100.4 3.1 %final_update.1 = (f32[4,32,1024]{2,1,0:T(8,128)}, f32[4,32]{1,0:T(4,128)}, f32[4,1024]{1,0:T(4,128)}, f32[32,512]{1,0:T(8,128)}, f32[1,32]{1,0:T(1,128)}, /*ind...) custom-call(f32[20,16,512]{2,1,0:T(8,128)S(1)} %get-tuple-element.42, ...), custom_call_target="tpu_custom_call" | custom-call | tf_op jit(solution)/shard_map/final_update/pallas_call | solution.py:459
